TPU v7x, 512 devices: a whole 4x8x8 slice. The times are simulated.
512 devices in a mesh: dp: 16 (over z, y_lo), comp: 32 (over y_hi, x, core).
Axes of the slice: x: 4, y: 8 (y_hi: 4, y_lo: 2; y = y_hi * 2 + y_lo), z: 8, core: 2. Of those that a mesh axis runs over, the one named last changes fastest.
Arguments:
- vectors: bfloat16 [2048, 256], P('dp'), may hold values from -8 to 8
- centers: float32 [512, 256], P('comp'), may hold values from -1.5 to 1.5
- factors: bfloat16 [512, 256, 256], P('comp', 'dp'), may hold values from -1 to 9.065873, as said below
- mixing: float32 [512], P('comp'), may hold values from 0.0005859375 to 0.005859375
Outputs:
- new_factors: float32 [512, 256, 256], P('comp', 'dp')
- new_means: float32 [512, 256], P('comp')
- new_weights: float32 [512], P('comp')
- evidence: float32 [2048], P('dp')
Inputs may be any that keep to these rules, and one draw needn't show every extreme that they name: `factors`: each component's 256 x 256 factor is lower triangular with a positive diagonal.
All inputs are finite; a program needn't handle non-finite values.
Results may differ from a plain program's by a relative error of at most 0.0003.
Values may be sent and summed in bfloat16 or wider, within the bound.
No kernel may reach another device: no remote copies, remote signals or barrier semaphores. Data moves between devices by JAX's collectives and lax.ppermute only.
A program may use at most 64 MiB of HBM per device.

v0:
```python
import math

import jax
import jax.numpy as jnp
from jax import lax
from jax.sharding import PartitionSpec as P

anneal = 1.0
step_weight = 0.5
ridge_term = 0.01
normal_offset = 0.9189385332046727
exact_mode = lax.Precision.HIGHEST


def sent_to_all(shard, axis):
    copies = jnp.broadcast_to(shard, (lax.axis_size(axis), *shard.shape))
    return lax.all_to_all(copies, axis, split_axis=0, concat_axis=0, tiled=True)


def of_everyone(shard, axis):
    everything = sent_to_all(shard, axis)
    return jnp.max(everything, axis=0)


def taken_together(shard, axis):
    return sent_to_all(shard, axis).sum(axis=0)


def in_order(tiles, dim):
    lengths = list(tiles.shape[1:])
    lengths[dim] *= tiles.shape[0]
    return jnp.moveaxis(tiles, 0, dim).reshape(lengths)


def gather_directly(shard, axis, dim):
    tiles = sent_to_all(shard, axis)
    return in_order(tiles, dim)


def in_blocks(shard, dim, peers):
    lengths = shard.shape
    tiles = shard.reshape(*lengths[:dim], peers, lengths[dim] // peers, *lengths[dim + 1 :])
    return jnp.moveaxis(tiles, dim, 0)


def summed_on_arrival(shard, axis, dim):
    tiles = in_blocks(shard, dim, lax.axis_size(axis))
    arrived = lax.all_to_all(tiles, axis, split_axis=0, concat_axis=0, tiled=True)
    return arrived.sum(axis=0)


def normalize(density, mixing, features):
    scores = anneal * (density + jnp.log(mixing)[:, None] - features * normal_offset)
    row_max = jnp.max(scores, axis=0)
    joined_max = of_everyone(row_max, "comp")
    joined_total = taken_together(jnp.sum(jnp.exp(scores - joined_max[None, :]), axis=0), "comp")
    shares = jnp.exp(scores - joined_max[None, :]) / joined_total[None, :]
    evidence = (joined_max + jnp.log(joined_total)) / anneal
    return (shares, evidence)


def refactor(pieces):
    scaled, moment_part = pieces
    identity = jnp.eye(scaled.shape[-1], dtype=jnp.float32)
    inverse = lax.linalg.triangular_solve(scaled, identity, left_side=True, lower=True)
    covariance = (
        jnp.dot(inverse, inverse.T, precision=exact_mode) + moment_part + ridge_term * identity
    )
    cholesky_factor = jnp.linalg.cholesky(covariance)
    return lax.linalg.triangular_solve(cholesky_factor, identity, left_side=True, lower=True)


def local(vectors, centers, factors, mixing):
    comp_count, row_count, features = factors.shape
    groups = lax.axis_size("dp")
    owned_count = comp_count // groups
    position = lax.axis_index("dp")
    row_start = position * row_count
    everyone = gather_directly(vectors, "dp", 0)
    vector_total = everyone.shape[0]
    block_rows = math.gcd(vector_total, 512)
    block_count = vector_total // block_rows
    shifted = jnp.einsum("krd,kd->kr", factors.astype(jnp.float32), centers, precision=exact_mode)
    diag_block = lax.dynamic_slice_in_dim(factors, row_start, row_count, 2).astype(jnp.float32)
    log_diag = jnp.sum(jnp.log(jnp.diagonal(diag_block, axis1=1, axis2=2)), axis=1)
    flattened = factors.reshape(comp_count * row_count, features)
    vector_blocks = everyone.reshape(block_count, block_rows, features)

    def density_block(vector_block):
        whitened = lax.dot_general(
            flattened, vector_block, (((1,), (1,)), ((), ())), preferred_element_type=jnp.float32
        )
        whitened = whitened.reshape(comp_count, row_count, -1) - shifted[:, :, None]
        return log_diag[:, None] - 0.5 * jnp.sum(whitened * whitened, axis=1)

    partial_density = (
        lax.map(density_block, vector_blocks).transpose(1, 0, 2).reshape(comp_count, vector_total)
    )
    density = summed_on_arrival(partial_density, "dp", 1)
    shares_local, evidence = normalize(density, mixing, features)
    shares_all = gather_directly(shares_local, "dp", 1)
    share_blocks = shares_all.reshape(comp_count, block_count, block_rows).transpose(1, 0, 2)

    def accumulate(running, inputs):
        first_sum, gram_sum = running
        vector_block, share_block = inputs
        wide_block = vector_block.astype(jnp.float32)
        first_sum = first_sum + jnp.dot(share_block, wide_block, precision=exact_mode)
        own_share = lax.dynamic_slice_in_dim(share_block, position * owned_count, owned_count, 0)
        weighted = own_share[:, None, :] * wide_block.T[None]
        weighted = weighted.reshape(owned_count * features, -1)
        gram_term = jnp.dot(weighted, wide_block, precision=exact_mode)
        return ((first_sum, gram_sum + gram_term), None)

    gram_start = jnp.zeros((owned_count * features, features), jnp.float32)
    first_start = jnp.zeros((comp_count, features), jnp.float32)
    (first_moment, gram_sum), unused = lax.scan(
        accumulate, (first_start, gram_start), (vector_blocks, share_blocks)
    )
    counts = jnp.sum(shares_all, axis=1)
    kept_share = (1.0 - step_weight) * mixing
    new_weights = kept_share + step_weight * counts / vector_total
    new_means = (
        kept_share[:, None] * centers + step_weight * first_moment / vector_total
    ) / new_weights[:, None]
    retained = kept_share / new_weights
    own_start = position * owned_count
    kept_own = lax.dynamic_slice_in_dim(kept_share, own_start, owned_count, 0)
    weight_own = lax.dynamic_slice_in_dim(new_weights, own_start, owned_count, 0)
    retained_own = lax.dynamic_slice_in_dim(retained, own_start, owned_count, 0)
    center_own = lax.dynamic_slice_in_dim(centers, own_start, owned_count, 0)
    mean_own = lax.dynamic_slice_in_dim(new_means, own_start, owned_count, 0)
    gram_own = gram_sum.reshape(owned_count, features, features)
    moment_part = (
        kept_own[:, None, None] * center_own[:, :, None] * center_own[:, None, :]
        + step_weight * gram_own / vector_total
    ) / weight_own[:, None, None] - mean_own[:, :, None] * mean_own[:, None, :]
    whole_factors = lax.all_to_all(
        factors.reshape(groups, owned_count, row_count, features),
        "dp",
        split_axis=0,
        concat_axis=2,
        tiled=True,
    )
    scaled = whole_factors[0].astype(jnp.float32) * lax.rsqrt(retained_own)[:, None, None]
    refreshed = lax.map(refactor, (scaled, moment_part))
    new_factors = lax.all_to_all(
        refreshed[None], "dp", split_axis=2, concat_axis=0, tiled=True
    ).reshape(comp_count, row_count, features)
    return (new_factors, new_means, new_weights, evidence)


def solution(mesh):
    return jax.shard_map(
        local,
        mesh=mesh,
        in_specs=(P("dp", None), P("comp", None), P("comp", "dp", None), P("comp")),
        out_specs=(P("comp", "dp", None), P("comp", None), P("comp"), P("dp")),
        check_vma=False,
    )
```

profile of v0, /device:TPU:8, one launch (start us, length us, event | category | flops | bytes accessed | tf_op | source)
XLA Modules:
  0.0 226.2 jit_solution(829906853297270123)
XLA Ops:
  0.6 1.9 broadcast_in_dim.32
  2.6 11.8 %all-to-all-start.1 = ((bf16[16,128,256]{2,1,0:T(8,128)(2,1)}), bf16[16,128,256]{2,1,0:T(8,128)(2,1)S(1)}, u32[]{:S(2)}, u32[]{:S(2)}) async-start(bf16[16,128,256]{2,1,0:T(8,128)(2,1)} %broadcast_in_dim.32), calls=%async_computation.1 | async-start | bytes 2097152 | tf_op jit(solution)/shard_map/all_to_all | solution.py:17
  17.3 24.4 %all-to-all-done.1 = bf16[16,128,256]{2,1,0:T(8,128)(2,1)S(1)} async-done(((bf16[16,128,256]{2,1,0:T(8,128)(2,1)}), bf16[16,128,256]{2,1,0:T(8,128)(2,1)S(1)}, u32[]{:S(2)}, u32[]{:S(2)}) %all-to-all-start.1) | async-done | bytes 1048608 | tf_op jit(solution)/shard_map/all_to_all | solution.py:17
  41.7 5.2 %while.34 = (s32[]{:T(128)}, f32[4,16,512]{2,1,0:T(8,128)S(1)}, f32[16]{0:T(128)S(1)}, bf16[4,512,256]{2,1,0:T(8,128)(2,1)S(1)}, bf16[256,256]{1,0:T(8,128)(2,1)}, /*index=5*/f32[16,16]{1,0:T(8,128)S(1)}, s32[]{:T(128)}) while((s32[]{:T(128)}, f32[4,16,512]{2,1,0:T(8,128)S(1)}, f32[16]{0:T(128)S(1)}, bf16[4,512,256]{2,1,0:T(8,128)(2,1)S(1)}, ...), condition=%wide.region_3.4_spmd, body=%wide.region_1.3_spmd.sunk | while | flops 67510272 | bytes 500309 | solution.py:97
  47.7 4.5 %all-to-all-start.2 = ((f32[16,16,128]{2,1,0:T(8,128)}), f32[16,16,128]{2,1,0:T(8,128)S(1)}, u32[]{:S(2)}, u32[]{:S(2)}) async-start(f32[16,16,128]{2,1,0:T(8,128)} %copy.58), calls=%async_computation.2 | async-start | bytes 262144 | tf_op jit(solution)/shard_map/all_to_all | solution.py:48
  52.2 8.5 %all-to-all-done.2 = f32[16,16,128]{2,1,0:T(8,128)S(1)} async-done(((f32[16,16,128]{2,1,0:T(8,128)}), f32[16,16,128]{2,1,0:T(8,128)S(1)}, u32[]{:S(2)}, u32[]{:S(2)}) %all-to-all-start.2) | async-done | bytes 131104 | tf_op jit(solution)/shard_map/all_to_all | solution.py:48
  60.8 18.6 %all_to_all.45 = f32[32,1,128]{2,1,0:T(1,128)S(1)} all-to-all(f32[32,1,128]{2,1,0:T(1,128)S(1)} %broadcast_in_dim.33), channel_id=1, replica_groups=mesh['dp'=16,'comp'=32] {'comp'}, dimensions={0} | all-to-all | bytes 32768 | tf_op jit(solution)/shard_map/all_to_all | solution.py:17
  79.6 12.8 %all_to_all.46 = f32[32,1,128]{2,1,0:T(1,128)S(1)} all-to-all(f32[32,1,128]{2,1,0:T(1,128)S(1)} %broadcast_in_dim.34), channel_id=1, replica_groups=mesh['dp'=16,'comp'=32] {'comp'}, dimensions={0} | all-to-all | bytes 32768 | tf_op jit(solution)/shard_map/all_to_all | solution.py:17
  93.1 4.0 %all-to-all-start.5 = ((f32[16,16,128]{2,1,0:T(8,128)}), f32[16,16,128]{2,1,0:T(8,128)S(1)}, u32[]{:S(2)}, u32[]{:S(2)}) async-start(f32[16,16,128]{2,1,0:T(8,128)} %broadcast_in_dim.35), calls=%async_computation.5 | async-start | bytes 262144 | tf_op jit(solution)/shard_map/all_to_all | solution.py:17
  97.2 8.5 %all-to-all-done.5 = f32[16,16,128]{2,1,0:T(8,128)S(1)} async-done(((f32[16,16,128]{2,1,0:T(8,128)}), f32[16,16,128]{2,1,0:T(8,128)S(1)}, u32[]{:S(2)}, u32[]{:S(2)}) %all-to-all-start.5) | async-done | bytes 131104 | tf_op jit(solution)/shard_map/all_to_all | solution.py:17
  105.7 4.3 %all-to-all-start = ((bf16[16,1,16,256]{3,2,1,0:T(8,128)(2,1)}), bf16[16,1,16,256]{3,2,1,0:T(8,128)(2,1)S(1)}, u32[]{:S(2)}, u32[]{:S(2)}) async-start(bf16[16,1,16,256]{3,2,1,0:T(8,128)(2,1)} %bitcast.4), calls=%async_computation | async-start | bytes 262144 | tf_op jit(solution)/shard_map/all_to_all | solution.py:138
  110.1 3.8 %while.35 = (s32[]{:T(128)}, f32[16,256]{1,0:T(8,128)S(1)}, f32[256,256]{1,0:T(8,128)S(1)}, f32[4,16,512]{2,1,0:T(8,128)S(1)}, bf16[4,512,256]{2,1,0:T(8,128)(2,...) while((s32[]{:T(128)}, f32[16,256]{1,0:T(8,128)S(1)}, f32[256,256]{1,0:T(8,128)S(1)}, ...), condition=%wide.region_11.13_spmd.clone, body=%wide.region_10.12_spmd.clone.sunk | while | flops 428220416 | bytes 1384576 | solution.py:117
  116.9 1.5 all-to-all-done
  118.6 4.0 %while.36 = (s32[]{:T(128)}, f32[256,256]{1,0:T(8,128)S(1)}, s32[2,2]{1,0:T(2,128)S(1)}, f32[2,128,128]{2,1,0:T(8,128)S(1)}, s32[]{:T(128)}) while((s32[]{:T(128)}, f32[256,256]{1,0:T(8,128)S(1)}, s32[2,2]{1,0:T(2,128)S(1)}, f32[2,128,128]{2,1,0:T(8,128)S(1)}, s32[]{:T(128)}) %tuple.98), condition=%wide.while_cond, body=%wide.while_body.sunk | while | flops 2 | bytes 131181 | solution.py:65
  122.6 19.9 %custom-call.23 = f32[2,128,128]{1,2,0:T(8,128)S(1)} custom-call(f32[2,128,128]{2,1,0:T(8,128)S(1)} %get-tuple-element.199), custom_call_target="InvertDiagBlocksLowerTriangular" | custom-call | tf_op jit(solution)/shard_map/while/body/eval_jaxpr/triangular_solve/custom-call.0 | solution.py:65
  145.4 11.7 %cholesky.49 = f32[128,128]{1,0:T(8,128)S(1)} custom-call(f32[128,128]{1,0:T(8,128)S(1)} %cholesky.115), custom_call_target="Cholesky" | custom-call | tf_op jit(solution)/shard_map/while/body/eval_jaxpr/jit(cholesky)/cholesky | solution.py:69
  157.1 9.8 %custom-call.17 = f32[1,128,128]{1,2,0:T(8,128)S(1)} custom-call(f32[1,128,128]{2,1,0:T(8,128)S(1)} %get-tuple-element.292), custom_call_target="InvertDiagBlocksLowerTriangular" | custom-call | tf_op jit(solution)/shard_map/while/body/eval_jaxpr/jit(cholesky)/cholesky | solution.py:69
  167.4 11.7 %cholesky.103 = f32[128,128]{1,0:T(8,128)S(1)} custom-call(f32[128,128]{1,0:T(8,128)S(1)} %convolution_subtract_fusion.2), custom_call_target="Cholesky" | custom-call | tf_op jit(solution)/shard_map/while/body/eval_jaxpr/jit(cholesky)/cholesky | solution.py:69
  182.3 4.3 %while.37 = (s32[]{:T(128)}, f32[256,256]{0,1:T(8,128)S(1)}, s32[2,2]{1,0:T(2,128)S(1)}, f32[2,128,128]{2,1,0:T(8,128)S(1)}, s32[]{:T(128)}) while((s32[]{:T(128)}, f32[256,256]{0,1:T(8,128)S(1)}, s32[2,2]{1,0:T(2,128)S(1)}, f32[2,128,128]{2,1,0:T(8,128)S(1)}, s32[]{:T(128)}) %tuple.110), condition=%wide.while_cond.clone, body=%wide.while_body.clone.sunk | while | flops 2 | bytes 393321 | solution.py:70
  182.9 1.4 dynamic-slice.21
  185.1 1.4 dynamic-slice.21
  186.6 19.9 %custom-call.24 = f32[2,128,128]{1,2,0:T(8,128)S(1)} custom-call(f32[2,128,128]{2,1,0:T(8,128)S(1)} %get-tuple-element.200), custom_call_target="InvertDiagBlocksLowerTriangular" | custom-call | tf_op jit(solution)/shard_map/while/body/eval_jaxpr/triangular_solve/custom-call.0 | solution.py:70
  208.6 7.2 %all-to-all-start.6 = ((f32[1,1,256,256]{3,1,0,2:T(1,128)}), f32[1,1,256,256]{3,1,0,2:T(1,128)S(1)}, u32[]{:S(2)}, u32[]{:S(2)}) async-start(f32[1,1,256,256]{3,1,0,2:T(1,128)} %copy.72), calls=%async_computation.6 | async-start | bytes 524288 | tf_op jit(solution)/shard_map/all_to_all | solution.py:147
  216.3 9.2 %all-to-all-done.6 = f32[1,1,256,256]{3,1,0,2:T(1,128)S(1)} async-done(((f32[1,1,256,256]{3,1,0,2:T(1,128)}), f32[1,1,256,256]{3,1,0,2:T(1,128)S(1)}, u32[]{:S(2)}, u32[]{:S(2)}) %all-to-all-start.6) | async-done | bytes 262176 | tf_op jit(solution)/shard_map/all_to_all | solution.py:147
  (111 shorter events, 29.8 us)
Async XLA Ops:
  2.6 39.1 %all-to-all-start.1 = ((bf16[16,128,256]{2,1,0:T(8,128)(2,1)}), bf16[16,128,256]{2,1,0:T(8,128)(2,1)S(1)}, u32[]{:S(2)}, u32[]{:S(2)}) async-start(bf16[16,128,256]{2,1,0:T(8,128)(2,1)} %broadcast_in_dim.32), calls=%async_computation.1 | async-start | bytes 2097152 | tf_op jit(solution)/shard_map/all_to_all | solution.py:17
  15.5 0.7 copy-start
  47.7 4.5 %copy-start.3 = (f32[16]{0:T(128)S(1)}, f32[16]{0:T(128)}, u32[]{:S(2)}) copy-start(f32[16]{0:T(128)} %param.13) | copy-start | bytes 196
  47.7 13.0 %all-to-all-start.2 = ((f32[16,16,128]{2,1,0:T(8,128)}), f32[16,16,128]{2,1,0:T(8,128)S(1)}, u32[]{:S(2)}, u32[]{:S(2)}) async-start(f32[16,16,128]{2,1,0:T(8,128)} %copy.58), calls=%async_computation.2 | async-start | bytes 262144 | tf_op jit(solution)/shard_map/all_to_all | solution.py:48
  93.1 12.6 %all-to-all-start.5 = ((f32[16,16,128]{2,1,0:T(8,128)}), f32[16,16,128]{2,1,0:T(8,128)S(1)}, u32[]{:S(2)}, u32[]{:S(2)}) async-start(f32[16,16,128]{2,1,0:T(8,128)} %broadcast_in_dim.35), calls=%async_computation.5 | async-start | bytes 262144 | tf_op jit(solution)/shard_map/all_to_all | solution.py:17
  105.7 12.7 %all-to-all-start = ((bf16[16,1,16,256]{3,2,1,0:T(8,128)(2,1)}), bf16[16,1,16,256]{3,2,1,0:T(8,128)(2,1)S(1)}, u32[]{:S(2)}, u32[]{:S(2)}) async-start(bf16[16,1,16,256]{3,2,1,0:T(8,128)(2,1)} %bitcast.4), calls=%async_computation | async-start | bytes 262144 | tf_op jit(solution)/shard_map/all_to_all | solution.py:138
  114.2 2.7 %copy-start.2 = (f32[16]{0:T(128)}, f32[16]{0:T(128)S(1)}, u32[]{:S(2)}) copy-start(f32[16]{0:T(128)S(1)} %get-tuple-element.286) | copy-start | bytes 196
  116.9 1.6 copy-start.1
  208.6 16.9 %all-to-all-start.6 = ((f32[1,1,256,256]{3,1,0,2:T(1,128)}), f32[1,1,256,256]{3,1,0,2:T(1,128)S(1)}, u32[]{:S(2)}, u32[]{:S(2)}) async-start(f32[1,1,256,256]{3,1,0,2:T(1,128)} %copy.72), calls=%async_computation.6 | async-start | bytes 524288 | tf_op jit(solution)/shard_map/all_to_all | solution.py:147
where the time goes:
time: 227 us; the launch traced here: 226 us
  other arithmetic  76.6 us (34%)
  waiting for transfers between devices  52.1 us (23%)
  starting transfers between devices  31.7 us (14%)
  blocking collectives  31.4 us (14%)
  local copies, waits for them, and re-layouts  17.9 us (8%)
  matrix products  13.1 us (6%)
  between operations  3.05 us (1%)
    another operation x7, other arithmetic, refactor(): cholesky_factor = jnp.linalg.cholesky(covariance)  34.7 us
    all_to_all x2, waiting for transfers between devices, sent_to_all(): return lax.all_to_all(copies, axis, split_axis=0, concat_axis=0, tiled=True)  32.9 us
    all_to_all x2, blocking collectives, sent_to_all(): return lax.all_to_all(copies, axis, split_axis=0, concat_axis=0, tiled=True)  31.4 us
    another operation x2, other arithmetic, refactor(): lax.linalg.triangular_solve(cholesky_factor, identity, left_side=True, lo...  19.9 us
    another operation x3, other arithmetic, refactor(): lax.linalg.triangular_solve(scaled, identity, left_side=True, lower=True)  19.9 us
    all_to_all x2, starting transfers between devices, sent_to_all(): return lax.all_to_all(copies, axis, split_axis=0, concat_axis=0, tiled=True)  15.8 us
    all_to_all x1, waiting for transfers between devices, local(): lax.all_to_all(refreshed[None], 'dp', split_axis=2, concat_axis=0, tiled=...  9.18 us
    all_to_all x1, waiting for transfers between devices, summed_on_arrival(): lax.all_to_all(tiles, axis, split_axis=0, concat_axis=0, tiled=True)  8.49 us
  transfers between devices with their start and end apart: 5, of which 5 were waited for; matrix products, arithmetic and copies ran while one was open for 4% of the time, Pallas kernels for 0%

commit v1 on v0

v1 whole, which is shorter than its diff:
```python
import jax
import jax.numpy as jnp
from jax import lax
from jax.experimental import pallas as pl
from jax.experimental.pallas import tpu as pltpu
from jax.sharding import PartitionSpec as P

step_weight = 0.5
ridge_term = 0.01
normal_offset = 0.9189385332046727
exact_mode = lax.Precision.HIGHEST
PANEL = 32
SUB = 16
f32 = jnp.float32
bf16 = jnp.bfloat16


def in_vmem(count):
    return [pl.BlockSpec(memory_space=pltpu.VMEM)] * count


def call(body, out_shape, scalars, *args, scratch=(), flops=0):
    single = not isinstance(out_shape, (list, tuple))
    return pl.pallas_call(
        body,
        out_shape=out_shape,
        in_specs=[pl.BlockSpec(memory_space=pltpu.SMEM)] + in_vmem(len(args)),
        out_specs=in_vmem(1)[0] if single else in_vmem(len(out_shape)),
        scratch_shapes=list(scratch),
        cost_estimate=pl.CostEstimate(flops=flops, transcendentals=0, bytes_accessed=0),
    )(scalars, *args)


def shape(dims, dtype=f32):
    return jax.ShapeDtypeStruct(dims, dtype)


def eye_of(size):
    rows = lax.broadcasted_iota(jnp.int32, (size, size), 0)
    cols = lax.broadcasted_iota(jnp.int32, (size, size), 1)
    return rows, cols


def three_parts(wide):
    high = wide.astype(bf16)
    rest = wide - high.astype(f32)
    mid = rest.astype(bf16)
    low = (rest - mid.astype(f32)).astype(bf16)
    return high, mid, low


def spread_body(where_ref, vectors_ref, factors_ref, out_ref):
    half = vectors_ref[:, pl.ds(pl.multiple_of(where_ref[1] * 128, 128), 128)]
    for peer in range(out_ref.shape[0]):
        out_ref[peer, :128, :] = half
        out_ref[peer, 128:144, :] = factors_ref[peer, :, :128]
        out_ref[peer, 144:160, :] = factors_ref[peer, :, 128:]


def gather_factor(got_ref, factor_ref):
    for peer in range(16):
        factor_ref[16 * peer : 16 * peer + 16, :128] = got_ref[peer, 128:144, :]
        factor_ref[16 * peer : 16 * peer + 16, 128:] = got_ref[peer, 144:160, :]


def score_body(where_ref, got_ref, other_ref, centers_ref, mixing_ref, out_ref, factor_ref):
    position, core = where_ref[0], where_ref[1]
    gather_factor(got_ref, factor_ref)
    wide = factor_ref[...].astype(f32)
    center = centers_ref[pl.ds(position, 1), :]
    shifted = jnp.sum(wide * center, axis=1, keepdims=True)
    rows, cols = eye_of(256)
    diagonal = jnp.sum(jnp.where(rows == cols, wide, 0.0), axis=1, keepdims=True)
    log_diag = jnp.sum(jnp.log(diagonal), axis=0, keepdims=True)
    log_mix = jnp.log(mixing_ref[pl.ds(position, 1), :])
    mine = factor_ref[:, pl.ds(pl.multiple_of(core * 128, 128), 128)]
    rest = factor_ref[:, pl.ds(pl.multiple_of((1 - core) * 128, 128), 128)]
    over_lanes = (((1,), (1,)), ((), ()))
    for pair in range(8):
        ours = got_ref[2 * pair : 2 * pair + 2, :128, :].reshape(256, 128)
        theirs = other_ref[2 * pair : 2 * pair + 2, :128, :].reshape(256, 128)
        whitened = lax.dot_general(mine, ours, over_lanes, preferred_element_type=f32)
        whitened += lax.dot_general(rest, theirs, over_lanes, preferred_element_type=f32)
        whitened -= shifted
        density = log_diag - 0.5 * jnp.sum(whitened * whitened, axis=0, keepdims=True)
        scores = density + log_mix[:, :1] - 256 * normal_offset
        out_ref[2 * pair] = scores[:, :128]
        out_ref[2 * pair + 1] = scores[:, 128:]


def invert_body(where_ref, got_ref, out_ref, factor_ref, inverse_ref):
    gather_factor(got_ref, factor_ref)
    rows, cols = eye_of(256)
    factor = factor_ref[...]
    diagonal = jnp.sum(jnp.where(rows == cols, factor.astype(f32), 0.0), axis=1, keepdims=True)
    inverse_ref[...] = jnp.where(rows == cols, 1.0 / diagonal, 0.0)

    def double(level, unused):
        inverse = inverse_ref[...]
        below = (rows >> (level + 1) == cols >> (level + 1)) & (rows >> level > cols >> level)
        step = jnp.where(below, factor_ref[...].astype(f32), 0.0)
        moved = jnp.dot(inverse, step, precision=exact_mode, preferred_element_type=f32)
        inverse_ref[...] = inverse - jnp.dot(
            moved, inverse, precision=exact_mode, preferred_element_type=f32
        )
        return unused

    lax.fori_loop(0, 8, double, 0)
    inverse = inverse_ref[...]
    out_ref[...] = lax.dot_general(
        inverse, inverse, (((1,), (1,)), ((), ())), precision=exact_mode, preferred_element_type=f32
    )


def order_body(where_ref, got_ref, other_ref, plain_ref, turned_ref):
    core = where_ref[1]
    ours = pl.ds(pl.multiple_of(core * 128, 128), 128)
    theirs = pl.ds(pl.multiple_of((1 - core) * 128, 128), 128)
    for block in range(16):
        mine, rest = got_ref[block, :128, :], other_ref[block, :128, :]
        plain_ref[128 * block : 128 * block + 128, ours] = mine
        plain_ref[128 * block : 128 * block + 128, theirs] = rest
        turned_ref[block, ours, :] = mine.astype(f32).T.astype(bf16)
        turned_ref[block, theirs, :] = rest.astype(f32).T.astype(bf16)


def partial_body(where_ref, scores_ref, out_ref):
    scores = scores_ref[:, 0, :]
    top = jnp.max(scores, axis=0, keepdims=True)
    total = jnp.sum(jnp.exp(scores - top), axis=0, keepdims=True)
    both = jnp.concatenate([top, total], axis=0)
    for peer in range(out_ref.shape[0]):
        out_ref[peer] = both


def share_body(where_ref, scores_ref, pairs_ref, shares_ref, evidence_ref):
    tops, totals = pairs_ref[:, 0, :], pairs_ref[:, 1, :]
    top = jnp.max(tops, axis=0, keepdims=True)
    total = jnp.sum(totals * jnp.exp(tops - top), axis=0, keepdims=True)
    evidence_ref[...] = top + jnp.log(total)
    shares = jnp.exp(scores_ref[:, 0, :] - top) / total
    for peer in range(shares_ref.shape[0]):
        shares_ref[peer] = shares


def eliminate(left_ref, right_ref, out_ref):
    size, panel, sub = 256, PANEL, SUB
    tiles = panel // 8
    in_tile = lax.broadcasted_iota(jnp.int32, (8, 128), 0)
    for start in range(0, size, panel):
        stop = start + panel
        first = start // 128
        left_tiles = list(range(first, 2))
        right_tiles = list(range(0, (stop - 1) // 128 + 1))
        rows = [
            [left_ref[start + 8 * i : start + 8 * i + 8, 128 * t : 128 * t + 128] for i in range(tiles)]
            for t in left_tiles
        ] + [
            [right_ref[start + 8 * i : start + 8 * i + 8, 128 * t : 128 * t + 128] for i in range(tiles)]
            for t in right_tiles
        ]
        scale = [jnp.zeros((8, 128), f32) for i in range(tiles)]
        for begin in range(0, panel, sub):
            lane = start % 128 + begin
            columns = [
                {
                    i: jnp.broadcast_to(rows[0][i][:, lane + k : lane + k + 1], (8, 128))
                    for i in range((begin + k) // 8, tiles)
                }
                for k in range(sub)
            ]
            for k in range(sub):
                row = begin + k
                tile, place = row // 8, row % 8
                column = columns[k]
                pivot = jnp.broadcast_to(column[tile][place : place + 1, :], (8, 128))
                root = lax.rsqrt(pivot)
                weight = root * root
                ratio = {i: column[i] * weight for i in range(tile, tiles)}
                ratio[tile] = jnp.where(in_tile > place, ratio[tile], 0.0)
                scale[tile] = jnp.where(in_tile == place, root, scale[tile])
                for later in range(k + 1, sub):
                    other = begin + later
                    factor = jnp.broadcast_to(
                        column[other // 8][other % 8 : other % 8 + 1, :], (8, 128)
                    )
                    for i in range(other // 8, tiles):
                        columns[later][i] = columns[later][i] - ratio[i] * factor
                for group in rows:
                    base = jnp.broadcast_to(group[tile][place : place + 1, :], (8, 128))
                    for i in range(tile, tiles):
                        group[i] = group[i] - ratio[i] * base
        solved = [
            jnp.concatenate([group[i] * scale[i] for i in range(tiles)], axis=0) for group in rows
        ]
        left = solved[: len(left_tiles)]
        right = solved[len(left_tiles) :]
        for piece in range(panel // 16):
            block = start // 16 + piece
            for t in range(2):
                lanes = slice(128 * t, 128 * t + 128)
                if t in right_tiles:
                    out_ref[block, :, lanes] = right[t][16 * piece : 16 * piece + 16, :]
                else:
                    out_ref[block, :, lanes] = jnp.zeros((16, 128), f32)
        if stop == size:
            break
        if stop % 128 == 0:
            left, left_tiles = left[1:], left_tiles[1:]
        wide = jnp.concatenate(left, axis=1)
        high, mid, low = three_parts(wide)
        turned = jnp.concatenate([high, high, mid, high, low, mid], axis=0)
        whole = jnp.concatenate(left + right, axis=1)
        high, mid, low = three_parts(whole)
        straight = jnp.concatenate([high, mid, high, low, high, mid], axis=0)
        change = lax.dot_general(
            turned, straight, (((0,), (0,)), ((), ())), preferred_element_type=f32
        )
        skip = stop - 128 * left_tiles[0]
        for position, t in enumerate(left_tiles):
            lanes = slice(128 * t, 128 * t + 128)
            left_ref[stop:, lanes] -= change[skip:, 128 * position : 128 * position + 128]
        for position, t in enumerate(right_tiles):
            lanes = slice(128 * t, 128 * t + 128)
            position += len(left_tiles)
            right_ref[stop:, lanes] -= change[skip:, 128 * position : 128 * position + 128]


def refactor_body(
    where_ref, shares_ref, plain_ref, turned_ref, square_ref, centers_ref, mixing_ref,
    out_ref, left_ref, right_ref,
):
    position = where_ref[0]
    vector_total = plain_ref.shape[0]
    share = shares_ref[:, pl.ds(position, 1), :].reshape(16, 128)
    gram = jnp.zeros((256, 256), f32)
    moment = jnp.zeros((256, 128), f32)
    for pair in range(8):
        weighted = []
        for block in (2 * pair, 2 * pair + 1):
            weighted.append(turned_ref[block].astype(f32) * share[block : block + 1, :])
            moment += weighted[-1]
        vectors = plain_ref[256 * pair : 256 * pair + 256, :]
        for part in three_parts(jnp.concatenate(weighted, axis=1)):
            gram += jnp.dot(part, vectors, preferred_element_type=f32)
    counts = jnp.sum(jnp.sum(share, axis=1, keepdims=True), axis=0, keepdims=True)
    moment = jnp.sum(moment, axis=1, keepdims=True)
    rows, cols = eye_of(256)
    same = rows == cols
    prior = mixing_ref[pl.ds(position, 1), :][:, :1]
    kept = (1.0 - step_weight) * prior
    weight = kept + step_weight * counts / vector_total
    center = centers_ref[pl.ds(position, 1), :]
    center_down = jnp.sum(jnp.where(same, center, 0.0), axis=1, keepdims=True)
    mean_down = (kept * center_down + step_weight * moment / vector_total) / weight
    mean = jnp.sum(jnp.where(same, mean_down, 0.0), axis=0, keepdims=True)
    left_ref[...] = (
        (kept / weight) * square_ref[...]
        + ((kept * center_down) * center + (step_weight / vector_total) * gram) / weight
        - mean_down * mean
        + jnp.where(same, ridge_term, 0.0)
    )
    right_ref[...] = jnp.where(same, 1.0, 0.0)
    eliminate(left_ref, right_ref, out_ref)


def means_body(where_ref, shares_ref, plain_ref, centers_ref, mixing_ref, means_ref, weights_ref):
    vector_total = plain_ref.shape[0]
    moment = jnp.zeros((16, 256), f32)
    counts = jnp.zeros((16, 128), f32)
    for block in range(16):
        share = shares_ref[block]
        counts += share
        vectors = plain_ref[128 * block : 128 * block + 128, :]
        for part in three_parts(share):
            moment += jnp.dot(part, vectors, preferred_element_type=f32)
    counts = jnp.sum(counts, axis=1, keepdims=True)
    kept = (1.0 - step_weight) * mixing_ref[...]
    weights = kept + step_weight * counts / vector_total
    weights_ref[...] = weights
    means_ref[...] = (
        kept[:, :1] * centers_ref[...] + step_weight * moment / vector_total
    ) / weights[:, :1]


def exchanged(array, axis):
    return lax.all_to_all(array, axis, split_axis=0, concat_axis=0, tiled=True)


def local(vectors, centers, factors, mixing):
    groups, peers = lax.axis_size("dp"), lax.axis_size("comp")
    where = jnp.stack([lax.axis_index("dp"), lax.axis_index("comp") % 2]).astype(jnp.int32)
    mixing_wide = jnp.broadcast_to(mixing[:, None], (16, 128))
    spread = call(spread_body, shape((groups, 160, 128), bf16), where, vectors, factors)
    got = exchanged(spread, "dp")
    other = lax.ppermute(got, "comp", [(i, i ^ 1) for i in range(peers)])
    scores = call(
        score_body, shape((16, 1, 128)), where, got, other, centers, mixing_wide,
        scratch=[pltpu.VMEM((256, 256), bf16)], flops=1 << 29,
    )
    scores_here = exchanged(scores, "dp")
    square = call(
        invert_body, shape((256, 256)), where, got,
        scratch=[pltpu.VMEM((256, 256), bf16), pltpu.VMEM((256, 256), f32)], flops=1 << 32,
    )
    plain, turned = call(
        order_body, [shape((2048, 256), bf16), shape((16, 256, 128), bf16)], where, got, other,
        flops=1 << 30,
    )
    partial = call(partial_body, shape((peers, 2, 128)), where, scores_here)
    pairs = exchanged(partial, "comp")
    shares, evidence = call(
        share_body, [shape((groups, 16, 128)), shape((1, 128))], where, scores_here, pairs
    )
    shares_all = exchanged(shares, "dp")
    refreshed = call(
        refactor_body, shape((16, 16, 256)), where, shares_all, plain, turned, square, centers,
        mixing_wide, scratch=[pltpu.VMEM((256, 256), f32)] * 2, flops=1 << 32,
    )
    new_factors = exchanged(refreshed, "dp")
    new_means, new_weights = call(
        means_body, [shape((16, 256)), shape((16, 128))], where, shares_all, plain, centers,
        mixing_wide, flops=1 << 28,
    )
    return new_factors, new_means, new_weights[:, 0], evidence.reshape(128)


def solution(mesh):
    return jax.shard_map(
        local,
        mesh=mesh,
        in_specs=(P("dp", None), P("comp", None), P("comp", "dp", None), P("comp")),
        out_specs=(P("comp", "dp", None), P("comp", None), P("comp"), P("dp")),
        check_vma=False,
    )
```

time: 227 us -> 125 us (0.55)
  other arithmetic: 76.6 us -> 0.59 us
  waiting for transfers between devices: 52.1 us -> 8.83 us
  Pallas kernels: 0 us -> 33.9 us
  blocking collectives: 31.4 us -> 61.7 us
  starting transfers between devices: 31.7 us -> 14.7 us
  local copies, waits for them, and re-layouts: 17.9 us -> 3.54 us
  matrix products: 13.1 us -> 0 us
  between operations: 3.05 us -> 0.66 us
    another operation x12 -> x1, other arithmetic: 74.5 us -> 0.59 us  [local(): jnp.stack([lax.axis_index('dp'), lax.axis_index('comp') % 2])]
    all_to_all x5 -> x2, waiting for transfers between devices: 52.1 us -> 6.77 us  [exchanged(): return lax.all_to_all(array, axis, split_axis=0, concat_axis=0, tiled=True)]
    pallas_call x0 -> x8, Pallas kernels: none -> 33.9 us  [call(): pl.pallas_call(body, out_shape=out_shape, in_specs=[pl.BlockSpec(memory_s...]
    all_to_all x2 -> x3, blocking collectives: 31.4 us -> 61.7 us  [exchanged(): return lax.all_to_all(array, axis, split_axis=0, concat_axis=0, tiled=True)]
    all_to_all x5 -> x2, starting transfers between devices: 31.7 us -> 12.8 us  [exchanged(): return lax.all_to_all(array, axis, split_axis=0, concat_axis=0, tiled=True)]
    dot_general x14 -> x0, matrix products: 10.6 us -> none  [the longest x4 4.83 us: density_block(): lax.dot_general(flattened, vector_block, (((1,), (1,)), ((), ())), prefer...]
    another operation x28 -> x0, local copies, waits for them, and re-layouts: 8.69 us -> none  [the longest x10 4.26 us: refactor(): lax.linalg.triangular_solve(cholesky_factor, identity, left_side=True, lo...]
    dynamic_slice x9 -> x0, local copies, waits for them, and re-layouts: 2.94 us -> none  [the longest x1 0.93 us: local(): lax.dynamic_slice_in_dim(factors, row_start, row_count, 2)]
  transfers between devices with their start and end apart: 5 -> 3, of which waited for: 5 -> 2; matrix products, arithmetic and copies ran while one was open for 4% -> 1% of each run, Pallas kernels for 0% -> 13%
where the time goes in v1:
time: 125 us; the launch traced here: 124 us
  blocking collectives  61.7 us (49%)
  Pallas kernels  33.9 us (27%)
  starting transfers between devices  14.7 us (12%)
  waiting for transfers between devices  8.83 us (7%)
  local copies, waits for them, and re-layouts  3.54 us (3%)
    all_to_all x3, blocking collectives, exchanged(): return lax.all_to_all(array, axis, split_axis=0, concat_axis=0, tiled=True)  61.7 us
    pallas_call x8, Pallas kernels, call(): pl.pallas_call(body, out_shape=out_shape, in_specs=[pl.BlockSpec(memory_s...  33.9 us
    all_to_all x2, starting transfers between devices, exchanged(): return lax.all_to_all(array, axis, split_axis=0, concat_axis=0, tiled=True)  12.8 us
    all_to_all x2, waiting for transfers between devices, exchanged(): return lax.all_to_all(array, axis, split_axis=0, concat_axis=0, tiled=True)  6.77 us
  transfers between devices with their start and end apart: 3, of which 2 were waited for; matrix products, arithmetic and copies ran while one was open for 1% of the time, Pallas kernels for 13%

profile of v1, /device:TPU:8, one launch (start us, length us, event | category | flops | bytes accessed | tf_op | source)
XLA Modules:
  0.0 123.9 jit_solution(11986406950301587548)
XLA Ops:
  0.6 0.6 pad_add_fusion.where_ref
  1.2 1.9 %shard_map.75 = bf16[16,160,128]{2,1,0:T(8,128)(2,1)} custom-call(s32[2]{0:T(128)} %pad_add_fusion.where_ref, bf16[128,256]{1,0:T(8,128)(2,1)} %vectors_ref.1, bf16[16,16,256]{2,1,0:T(8,128)(2,1)} %factors_ref.1), custom_call_target="tpu_custom_call" | custom-call | tf_op jit(solution)/shard_map/pallas_call | solution.py:24
  3.1 31.4 %all_to_all.25.got_ref = bf16[16,160,128]{2,1,0:T(8,128)(2,1)S(1)} all-to-all(bf16[16,160,128]{2,1,0:T(8,128)(2,1)} %shard_map.75), channel_id=1, replica_groups=mesh['dp'=16,'comp'=32] {'dp'}, dimensions={0} | all-to-all | bytes 1310720 | tf_op jit(solution)/shard_map/all_to_all | solution.py:287
  34.5 1.9 %collective-permute-start = (bf16[16,160,128]{2,1,0:T(8,128)(2,1)S(1)}, bf16[16,160,128]{2,1,0:T(8,128)(2,1)S(1)}, u32[]{:S(2)}, u32[]{:S(2)}) collective-permute-start(bf16[16,160,128]{2,1,0:T(8,128)(2,1)S(1)} %all_to_all.25.got_ref), channel_id=1, source_target_pairs={{0,1},{1,0},{2,3},{3,2},{4,5},{5,4},{6,7},{7,6},{8,9},{9,8},{10,11... | collective-permute-start | bytes 1966088 | tf_op jit(solution)/shard_map/ppermute | solution.py:296
  36.4 2.1 %collective-permute-done.other_ref = bf16[16,160,128]{2,1,0:T(8,128)(2,1)S(1)} collective-permute-done((bf16[16,160,128]{2,1,0:T(8,128)(2,1)S(1)}, bf16[16,160,128]{2,1,0:T(8,128)(2,1)S(1)}, u32[]{:S(2)}, u32[]{:S(2)}) %collective-permute-start) | collective-permute-done | bytes 655392 | tf_op jit(solution)/shard_map/ppermute | solution.py:296
  38.5 0.0 copy-done.2
  38.5 0.8 broadcast_in_dim.2.mixing_ref
  39.2 0.1 copy-done.3
  39.3 2.7 %shard_map.76 = f32[16,1,128]{2,1,0:T(1,128)} custom-call(s32[2]{0:T(128)} %pad_add_fusion.where_ref, bf16[16,160,128]{2,1,0:T(8,128)(2,1)} %copy-done, bf16[16,160,128]{2,1,0:T(8,128)(2,1)} %copy-done.3, f32[16,256]{1,0:T(8,128)} %centers_ref.5, f32[16,128]{1,0:T(8,128)} %broadcast_in_dim.2.mixing_ref), custom_call_target="tpu_custom_call" | custom-call | flops 536870912 | tf_op jit(solution)/shard_map/pallas_call | solution.py:24
  42.0 11.3 %all_to_all.26.scores_ref = f32[16,1,128]{2,1,0:T(1,128)} all-to-all(f32[16,1,128]{2,1,0:T(1,128)} %shard_map.76), channel_id=1, replica_groups=mesh['dp'=16,'comp'=32] {'dp'}, dimensions={0} | all-to-all | bytes 16384 | tf_op jit(solution)/shard_map/all_to_all | solution.py:287
  53.3 1.4 %shard_map.77 = f32[32,2,128]{2,1,0:T(2,128)} custom-call(s32[2]{0:T(128)} %pad_add_fusion.where_ref, f32[16,1,128]{2,1,0:T(1,128)} %all_to_all.26.scores_ref), custom_call_target="tpu_custom_call" | custom-call | tf_op jit(solution)/shard_map/pallas_call | solution.py:24
  54.7 19.0 %all_to_all.27.pairs_ref = f32[32,2,128]{2,1,0:T(2,128)} all-to-all(f32[32,2,128]{2,1,0:T(2,128)} %shard_map.77), channel_id=1, replica_groups=mesh['dp'=16,'comp'=32] {'comp'}, dimensions={0} | all-to-all | bytes 65536 | tf_op jit(solution)/shard_map/all_to_all | solution.py:287
  73.7 1.5 %shard_map.78 = (f32[16,16,128]{2,1,0:T(8,128)}, f32[1,128]{1,0:T(1,128)}) custom-call(s32[2]{0:T(128)} %pad_add_fusion.where_ref, f32[16,1,128]{2,1,0:T(1,128)} %all_to_all.26.scores_ref, f32[32,2,128]{2,1,0:T(2,128)} %all_to_all.27.pairs_ref), custom_call_target="tpu_custom_call" | custom-call | tf_op jit(solution)/shard_map/pallas_call | solution.py:24
  75.2 4.6 %all-to-all-start.3 = ((f32[16,16,128]{2,1,0:T(8,128)}), f32[16,16,128]{2,1,0:T(8,128)S(1)}, u32[]{:S(2)}, u32[]{:S(2)}) async-start(f32[16,16,128]{2,1,0:T(8,128)} %get-tuple-element.10), calls=%async_computation.3 | async-start | bytes 262144 | tf_op jit(solution)/shard_map/all_to_all | solution.py:287
  79.8 10.8 %shard_map.80.square_ref = f32[256,256]{1,0:T(8,128)} custom-call(s32[2]{0:T(128)} %pad_add_fusion.where_ref, bf16[16,160,128]{2,1,0:T(8,128)(2,1)} %copy-done), custom_call_target="tpu_custom_call" | custom-call | flops 4294967296 | tf_op jit(solution)/shard_map/pallas_call | solution.py:24
  90.6 2.9 %shard_map.79 = (bf16[2048,256]{1,0:T(8,128)(2,1)}, bf16[16,256,128]{2,1,0:T(8,128)(2,1)}) custom-call(s32[2]{0:T(128)} %pad_add_fusion.where_ref, bf16[16,160,128]{2,1,0:T(8,128)(2,1)} %copy-done, bf16[16,160,128]{2,1,0:T(8,128)(2,1)} %copy-done.3), custom_call_target="tpu_custom_call" | custom-call | flops 1073741824 | tf_op jit(solution)/shard_map/pallas_call | solution.py:24
  93.5 0.0 all-to-all-done.3.shares_ref
  93.5 0.7 copy-done.1
  94.2 10.4 %shard_map.81 = f32[16,16,256]{2,1,0:T(8,128)} custom-call(s32[2]{0:T(128)} %pad_add_fusion.where_ref, f32[16,16,128]{2,1,0:T(8,128)} %copy-done.1, bf16[2048,256]{1,0:T(8,128)(2,1)} %get-tuple-element.11.plain_ref, bf16[16,256,128]{2,1,0:T(8,128)(2,1)} %get-tuple-element.12.turned_ref, f32[256,256]{1,0:T(8,128)} %shard_map.80.square_ref, ...), custom_call_target="tpu_custom_call" | custom-call | flops 4294967296 | tf_op jit(solution)/shard_map/pallas_call | solution.py:24
  104.6 8.2 %all-to-all-start.4 = ((f32[16,16,256]{2,1,0:T(8,128)}), f32[16,16,256]{2,1,0:T(8,128)S(1)}, u32[]{:S(2)}, u32[]{:S(2)}) async-start(f32[16,16,256]{2,1,0:T(8,128)} %shard_map.81), calls=%async_computation.4 | async-start | bytes 524288 | tf_op jit(solution)/shard_map/all_to_all | solution.py:287
  112.8 2.4 %shard_map.82 = (f32[16,256]{1,0:T(8,128)}, f32[16,128]{1,0:T(8,128)}) custom-call(s32[2]{0:T(128)} %pad_add_fusion.where_ref, f32[16,16,128]{2,1,0:T(8,128)} %copy-done.1, bf16[2048,256]{1,0:T(8,128)(2,1)} %get-tuple-element.11.plain_ref, f32[16,256]{1,0:T(8,128)} %centers_ref.5, f32[16,128]{1,0:T(8,128)} %broadcast_in_dim.2.mixing_ref), custom_call_target="tpu_custom_call" | custom-call | flops 268435456 | tf_op jit(solution)/shard_map/pallas_call | solution.py:24
  115.1 1.3 %slice_reduce_fusion = f32[16]{0:T(128)} fusion(f32[16,128]{1,0:T(8,128)} %get-tuple-element.14), kind=kLoop, calls=%fused_computation | loop fusion | bytes 128 | tf_op jit(solution)/shard_map/slice | solution.py:325
  116.5 6.8 %all-to-all-done.4 = f32[16,16,256]{2,1,0:T(8,128)S(1)} async-done(((f32[16,16,256]{2,1,0:T(8,128)}), f32[16,16,256]{2,1,0:T(8,128)S(1)}, u32[]{:S(2)}, u32[]{:S(2)}) %all-to-all-start.4) | async-done | bytes 262176 | tf_op jit(solution)/shard_map/all_to_all | solution.py:287
  123.2 0.7 copy.9
  (5 shorter events, 0.0 us)
Async XLA Ops:
  3.1 35.4 %copy-start.2 = (f32[16]{0:T(128)S(1)}, f32[16]{0:T(128)}, u32[]{:S(2)}) copy-start(f32[16]{0:T(128)} %param.7) | copy-start | bytes 196
  34.5 4.7 %copy-start = (bf16[16,160,128]{2,1,0:T(8,128)(2,1)}, bf16[16,160,128]{2,1,0:T(8,128)(2,1)S(1)}, u32[]{:S(2)}) copy-start(bf16[16,160,128]{2,1,0:T(8,128)(2,1)S(1)} %all_to_all.25.got_ref) | copy-start | bytes 1966084
  34.5 4.0 %collective-permute-start = (bf16[16,160,128]{2,1,0:T(8,128)(2,1)S(1)}, bf16[16,160,128]{2,1,0:T(8,128)(2,1)S(1)}, u32[]{:S(2)}, u32[]{:S(2)}) collective-permute-start(bf16[16,160,128]{2,1,0:T(8,128)(2,1)S(1)} %all_to_all.25.got_ref), channel_id=1, source_target_pairs={{0,1},{1,0},{2,3},{3,2},{4,5},{5,4},{6,7},{7,6},{8,9},{9,8},{10,11... | collective-permute-start | bytes 1966088 | tf_op jit(solution)/shard_map/ppermute | solution.py:296
  38.5 0.9 copy-start.3
  75.2 18.3 %all-to-all-start.3 = ((f32[16,16,128]{2,1,0:T(8,128)}), f32[16,16,128]{2,1,0:T(8,128)S(1)}, u32[]{:S(2)}, u32[]{:S(2)}) async-start(f32[16,16,128]{2,1,0:T(8,128)} %get-tuple-element.10), calls=%async_computation.3 | async-start | bytes 262144 | tf_op jit(solution)/shard_map/all_to_all | solution.py:287
  93.5 0.7 copy-start.1
  104.6 18.6 %all-to-all-start.4 = ((f32[16,16,256]{2,1,0:T(8,128)}), f32[16,16,256]{2,1,0:T(8,128)S(1)}, u32[]{:S(2)}, u32[]{:S(2)}) async-start(f32[16,16,256]{2,1,0:T(8,128)} %shard_map.81), calls=%async_computation.4 | async-start | bytes 524288 | tf_op jit(solution)/shard_map/all_to_all | solution.py:287

commit v2 on v1

--- a/solution.py
+++ b/solution.py
@@ -15,24 +15,37 @@
 bf16 = jnp.bfloat16
 
 
-def in_vmem(count):
-    return [pl.BlockSpec(memory_space=pltpu.VMEM)] * count
-
-
-def call(body, out_shape, scalars, *args, scratch=(), flops=0):
+def call(body, out_shape, *args, scratch=(), flops=0):
     single = not isinstance(out_shape, (list, tuple))
+    vmem = pl.BlockSpec(memory_space=pltpu.VMEM)
+    args = [pltpu.with_memory_space_constraint(arg, pltpu.VMEM) for arg in args]
     return pl.pallas_call(
         body,
         out_shape=out_shape,
-        in_specs=[pl.BlockSpec(memory_space=pltpu.SMEM)] + in_vmem(len(args)),
-        out_specs=in_vmem(1)[0] if single else in_vmem(len(out_shape)),
+        in_specs=[vmem] * len(args),
+        out_specs=vmem if single else [vmem] * len(out_shape),
         scratch_shapes=list(scratch),
         cost_estimate=pl.CostEstimate(flops=flops, transcendentals=0, bytes_accessed=0),
-    )(scalars, *args)
+        compiler_params=pltpu.CompilerParams(vmem_limit_bytes=12 << 20),
+    )(*args)
+
+
+def place():
+    return lax.axis_index("dp"), lax.axis_index("comp") % 2
 
 
 def shape(dims, dtype=f32):
+    return pltpu.VMEM(dims, dtype)
+
+
+def far(dims, dtype=f32):
     return jax.ShapeDtypeStruct(dims, dtype)
+
+
+def own_of(row_ref, position):
+    row = row_ref[...]
+    lanes = lax.broadcasted_iota(jnp.int32, row.shape, 1)
+    return jnp.sum(jnp.where(lanes == position, row, 0.0), axis=1, keepdims=True)
 
 
 def eye_of(size):
@@ -49,8 +62,9 @@
     return high, mid, low
 
 
-def spread_body(where_ref, vectors_ref, factors_ref, out_ref):
-    half = vectors_ref[:, pl.ds(pl.multiple_of(where_ref[1] * 128, 128), 128)]
+def spread_body(vectors_ref, factors_ref, out_ref):
+    unused, core = place()
+    half = vectors_ref[:, pl.ds(pl.multiple_of(core * 128, 128), 128)]
     for peer in range(out_ref.shape[0]):
         out_ref[peer, :128, :] = half
         out_ref[peer, 128:144, :] = factors_ref[peer, :, :128]
@@ -63,8 +77,8 @@
         factor_ref[16 * peer : 16 * peer + 16, 128:] = got_ref[peer, 144:160, :]
 
 
-def score_body(where_ref, got_ref, other_ref, centers_ref, mixing_ref, out_ref, factor_ref):
-    position, core = where_ref[0], where_ref[1]
+def score_body(got_ref, other_ref, centers_ref, mixing_ref, out_ref, factor_ref):
+    position, core = place()
     gather_factor(got_ref, factor_ref)
     wide = factor_ref[...].astype(f32)
     center = centers_ref[pl.ds(position, 1), :]
@@ -72,7 +86,7 @@
     rows, cols = eye_of(256)
     diagonal = jnp.sum(jnp.where(rows == cols, wide, 0.0), axis=1, keepdims=True)
     log_diag = jnp.sum(jnp.log(diagonal), axis=0, keepdims=True)
-    log_mix = jnp.log(mixing_ref[pl.ds(position, 1), :])
+    log_mix = jnp.log(own_of(mixing_ref, position))
     mine = factor_ref[:, pl.ds(pl.multiple_of(core * 128, 128), 128)]
     rest = factor_ref[:, pl.ds(pl.multiple_of((1 - core) * 128, 128), 128)]
     over_lanes = (((1,), (1,)), ((), ()))
@@ -83,37 +97,46 @@
         whitened += lax.dot_general(rest, theirs, over_lanes, preferred_element_type=f32)
         whitened -= shifted
         density = log_diag - 0.5 * jnp.sum(whitened * whitened, axis=0, keepdims=True)
-        scores = density + log_mix[:, :1] - 256 * normal_offset
+        scores = density + log_mix - 256 * normal_offset
         out_ref[2 * pair] = scores[:, :128]
         out_ref[2 * pair + 1] = scores[:, 128:]
 
 
-def invert_body(where_ref, got_ref, out_ref, factor_ref, inverse_ref):
+def apart(left, right, **options):
+    return jnp.dot(left, right, precision=exact_mode, preferred_element_type=f32)
+
+
+def invert_body(got_ref, out_ref, factor_ref, inverse_ref):
     gather_factor(got_ref, factor_ref)
-    rows, cols = eye_of(256)
-    factor = factor_ref[...]
-    diagonal = jnp.sum(jnp.where(rows == cols, factor.astype(f32), 0.0), axis=1, keepdims=True)
-    inverse_ref[...] = jnp.where(rows == cols, 1.0 / diagonal, 0.0)
-
-    def double(level, unused):
-        inverse = inverse_ref[...]
+    rows, cols = eye_of(128)
+    factors = []
+    for start in (0, 128):
+        factor = factor_ref[start : start + 128, start : start + 128].astype(f32)
+        diagonal = jnp.sum(jnp.where(rows == cols, factor, 0.0), axis=1, keepdims=True)
+        factors.append(factor)
+        inverse_ref[start // 128] = jnp.where(rows == cols, 1.0 / diagonal, 0.0)
+    for level in range(7):
         below = (rows >> (level + 1) == cols >> (level + 1)) & (rows >> level > cols >> level)
-        step = jnp.where(below, factor_ref[...].astype(f32), 0.0)
-        moved = jnp.dot(inverse, step, precision=exact_mode, preferred_element_type=f32)
-        inverse_ref[...] = inverse - jnp.dot(
-            moved, inverse, precision=exact_mode, preferred_element_type=f32
-        )
-        return unused
-
-    lax.fori_loop(0, 8, double, 0)
-    inverse = inverse_ref[...]
+        for block in range(2):
+            inverse = inverse_ref[block]
+            step = jnp.where(below, factors[block], 0.0)
+            inverse_ref[block] = inverse - apart(apart(inverse, step), inverse)
+    first, last = inverse_ref[0], inverse_ref[1]
+    corner = -apart(apart(last, factor_ref[128:, :128].astype(f32)), first)
+    bottom = jnp.concatenate([corner, last], axis=1)
+    whole = jnp.concatenate(
+        [jnp.concatenate([first, jnp.zeros((128, 128), f32)], axis=1), bottom], axis=0
+    )
     out_ref[...] = lax.dot_general(
-        inverse, inverse, (((1,), (1,)), ((), ())), precision=exact_mode, preferred_element_type=f32
-    )
-
-
-def order_body(where_ref, got_ref, other_ref, plain_ref, turned_ref):
-    core = where_ref[1]
+        whole, whole, (((1,), (1,)), ((), ())), precision=exact_mode, preferred_element_type=f32
+    )
+
+
+INV_SCRATCH = [pltpu.VMEM((256, 256), bf16), pltpu.VMEM((2, 128, 128), f32)]
+
+
+def order_body(got_ref, other_ref, plain_ref, turned_ref):
+    unused, core = place()
     ours = pl.ds(pl.multiple_of(core * 128, 128), 128)
     theirs = pl.ds(pl.multiple_of((1 - core) * 128, 128), 128)
     for block in range(16):
@@ -124,7 +147,12 @@
         turned_ref[block, theirs, :] = rest.astype(f32).T.astype(bf16)
 
 
-def partial_body(where_ref, scores_ref, out_ref):
+def prepare_body(got_ref, other_ref, square_ref, plain_ref, turned_ref, factor_ref, inverse_ref):
+    invert_body(got_ref, square_ref, factor_ref, inverse_ref)
+    order_body(got_ref, other_ref, plain_ref, turned_ref)
+
+
+def partial_body(scores_ref, out_ref):
     scores = scores_ref[:, 0, :]
     top = jnp.max(scores, axis=0, keepdims=True)
     total = jnp.sum(jnp.exp(scores - top), axis=0, keepdims=True)
@@ -133,7 +161,7 @@
         out_ref[peer] = both
 
 
-def share_body(where_ref, scores_ref, pairs_ref, shares_ref, evidence_ref):
+def share_body(scores_ref, pairs_ref, shares_ref, evidence_ref):
     tops, totals = pairs_ref[:, 0, :], pairs_ref[:, 1, :]
     top = jnp.max(tops, axis=0, keepdims=True)
     total = jnp.sum(totals * jnp.exp(tops - top), axis=0, keepdims=True)
@@ -227,10 +255,10 @@
 
 
 def refactor_body(
-    where_ref, shares_ref, plain_ref, turned_ref, square_ref, centers_ref, mixing_ref,
+    shares_ref, plain_ref, turned_ref, square_ref, centers_ref, mixing_ref,
     out_ref, left_ref, right_ref,
 ):
-    position = where_ref[0]
+    position, unused = place()
     vector_total = plain_ref.shape[0]
     share = shares_ref[:, pl.ds(position, 1), :].reshape(16, 128)
     gram = jnp.zeros((256, 256), f32)
@@ -247,7 +275,7 @@
     moment = jnp.sum(moment, axis=1, keepdims=True)
     rows, cols = eye_of(256)
     same = rows == cols
-    prior = mixing_ref[pl.ds(position, 1), :][:, :1]
+    prior = own_of(mixing_ref, position)
     kept = (1.0 - step_weight) * prior
     weight = kept + step_weight * counts / vector_total
     center = centers_ref[pl.ds(position, 1), :]
@@ -264,7 +292,7 @@
     eliminate(left_ref, right_ref, out_ref)
 
 
-def means_body(where_ref, shares_ref, plain_ref, centers_ref, mixing_ref, means_ref, weights_ref):
+def means_body(shares_ref, plain_ref, centers_ref, mixing_ref, means_ref, weights_ref):
     vector_total = plain_ref.shape[0]
     moment = jnp.zeros((16, 256), f32)
     counts = jnp.zeros((16, 128), f32)
@@ -275,12 +303,14 @@
         for part in three_parts(share):
             moment += jnp.dot(part, vectors, preferred_element_type=f32)
     counts = jnp.sum(counts, axis=1, keepdims=True)
-    kept = (1.0 - step_weight) * mixing_ref[...]
+    rows, cols = eye_of(16)
+    prior = jnp.sum(jnp.where(rows == cols, mixing_ref[...], 0.0), axis=1, keepdims=True)
+    kept = (1.0 - step_weight) * prior
     weights = kept + step_weight * counts / vector_total
-    weights_ref[...] = weights
+    weights_ref[...] = jnp.sum(jnp.where(rows == cols, weights, 0.0), axis=0, keepdims=True)
     means_ref[...] = (
-        kept[:, :1] * centers_ref[...] + step_weight * moment / vector_total
-    ) / weights[:, :1]
+        kept * centers_ref[...] + step_weight * moment / vector_total
+    ) / weights
 
 
 def exchanged(array, axis):
@@ -289,40 +319,40 @@
 
 def local(vectors, centers, factors, mixing):
     groups, peers = lax.axis_size("dp"), lax.axis_size("comp")
-    where = jnp.stack([lax.axis_index("dp"), lax.axis_index("comp") % 2]).astype(jnp.int32)
-    mixing_wide = jnp.broadcast_to(mixing[:, None], (16, 128))
-    spread = call(spread_body, shape((groups, 160, 128), bf16), where, vectors, factors)
+    priors = mixing.reshape(1, 16)
+    spread = call(spread_body, shape((groups, 160, 128), bf16), vectors, factors)
     got = exchanged(spread, "dp")
     other = lax.ppermute(got, "comp", [(i, i ^ 1) for i in range(peers)])
     scores = call(
-        score_body, shape((16, 1, 128)), where, got, other, centers, mixing_wide,
+        score_body, shape((16, 1, 128)), got, other, centers, priors,
         scratch=[pltpu.VMEM((256, 256), bf16)], flops=1 << 29,
     )
+    scores, after, after_other = lax.optimization_barrier((scores, got, other))
     scores_here = exchanged(scores, "dp")
-    square = call(
-        invert_body, shape((256, 256)), where, got,
-        scratch=[pltpu.VMEM((256, 256), bf16), pltpu.VMEM((256, 256), f32)], flops=1 << 32,
-    )
-    plain, turned = call(
-        order_body, [shape((2048, 256), bf16), shape((16, 256, 128), bf16)], where, got, other,
-        flops=1 << 30,
-    )
-    partial = call(partial_body, shape((peers, 2, 128)), where, scores_here)
+    square, plain, turned = call(
+        prepare_body,
+        [shape((256, 256)), shape((2048, 256), bf16), shape((16, 256, 128), bf16)],
+        after, after_other, scratch=INV_SCRATCH, flops=1 << 30,
+    )
+    scores_here, square, plain, turned = lax.optimization_barrier(
+        (scores_here, square, plain, turned)
+    )
+    partial = call(partial_body, shape((peers, 2, 128)), scores_here)
     pairs = exchanged(partial, "comp")
     shares, evidence = call(
-        share_body, [shape((groups, 16, 128)), shape((1, 128))], where, scores_here, pairs
+        share_body, [shape((groups, 16, 128)), far((1, 128))], scores_here, pairs
     )
     shares_all = exchanged(shares, "dp")
     refreshed = call(
-        refactor_body, shape((16, 16, 256)), where, shares_all, plain, turned, square, centers,
-        mixing_wide, scratch=[pltpu.VMEM((256, 256), f32)] * 2, flops=1 << 32,
+        refactor_body, shape((16, 16, 256)), shares_all, plain, turned, square, centers,
+        priors, scratch=[pltpu.VMEM((256, 256), f32)] * 2, flops=1 << 32,
     )
     new_factors = exchanged(refreshed, "dp")
     new_means, new_weights = call(
-        means_body, [shape((16, 256)), shape((16, 128))], where, shares_all, plain, centers,
-        mixing_wide, flops=1 << 28,
-    )
-    return new_factors, new_means, new_weights[:, 0], evidence.reshape(128)
+        means_body, [far((16, 256)), far((1, 16))], shares_all, plain, centers, priors,
+        flops=1 << 28,
+    )
+    return new_factors, new_means, new_weights.reshape(16), evidence.reshape(128)
 
 
 def solution(mesh):

time: 125 us -> 107 us (0.86)
  Pallas kernels: 33.9 us -> 15.5 us
  starting transfers between devices: 14.7 us -> 10 us
  waiting for transfers between devices: 8.83 us -> 13.2 us
  blocking collectives: 61.7 us -> 63.7 us
    pallas_call x8 -> x7, Pallas kernels: 33.9 us -> 15.5 us  [call(): pl.pallas_call(body, out_shape=out_shape, in_specs=[vmem] * len(args), ou...]
    all_to_all x2, starting transfers between devices: 12.8 us -> 7.98 us  [exchanged(): return lax.all_to_all(array, axis, split_axis=0, concat_axis=0, tiled=True)]
    all_to_all x2, waiting for transfers between devices: 6.77 us -> 11.2 us  [exchanged(): return lax.all_to_all(array, axis, split_axis=0, concat_axis=0, tiled=True)]
    all_to_all x3, blocking collectives: 61.7 us -> 63.7 us  [exchanged(): return lax.all_to_all(array, axis, split_axis=0, concat_axis=0, tiled=True)]
    unnamed x9 -> x13, local copies, waits for them, and re-layouts: 1.47 us -> 3.15 us
    slice x1 -> x0, local copies, waits for them, and re-layouts: 1.32 us -> none  [local(): return (new_factors, new_means, new_weights[:, 0], evidence.reshape(128))]
  transfers between devices with their start and end apart: 3 -> 3, of which waited for: 2 -> 3; matrix products, arithmetic and copies ran while one was open for 1% -> 0% of each run, Pallas kernels for 13% -> 5%
where the time goes in v2:
time: 107 us; the launch traced here: 106 us
  blocking collectives  63.7 us (60%)
  Pallas kernels  15.5 us (14%)
  waiting for transfers between devices  13.2 us (12%)
  starting transfers between devices  10 us (9%)
  local copies, waits for them, and re-layouts  3.15 us (3%)
    all_to_all x3, blocking collectives, exchanged(): return lax.all_to_all(array, axis, split_axis=0, concat_axis=0, tiled=True)  63.7 us
    pallas_call x7, Pallas kernels, call(): pl.pallas_call(body, out_shape=out_shape, in_specs=[vmem] * len(args), ou...  15.5 us
    all_to_all x2, waiting for transfers between devices, exchanged(): return lax.all_to_all(array, axis, split_axis=0, concat_axis=0, tiled=True)  11.2 us
    all_to_all x2, starting transfers between devices, exchanged(): return lax.all_to_all(array, axis, split_axis=0, concat_axis=0, tiled=True)  7.98 us
    unnamed x13, local copies, waits for them, and re-layouts  3.15 us
  transfers between devices with their start and end apart: 3, of which 3 were waited for; matrix products, arithmetic and copies ran while one was open for 0% of the time, Pallas kernels for 5%

profile of v2, /device:TPU:8, one launch (start us, length us, event | category | flops | bytes accessed | tf_op | source)
XLA Modules:
  0.0 106.3 jit_solution(714204811611739407)
XLA Ops:
  0.6 0.0 copy-start
  0.6 0.9 copy-done
  1.5 0.8 copy-done.1
  2.4 0.1 shard_map.75
  2.5 0.0 copy-start.2
  2.5 31.1 %all_to_all.25.got_ref = bf16[16,160,128]{2,1,0:T(8,128)(2,1)S(1)} all-to-all(bf16[16,160,128]{2,1,0:T(8,128)(2,1)S(1)} %shard_map.75), channel_id=1, replica_groups=mesh['dp'=16,'comp'=32] {'dp'}, dimensions={0} | all-to-all | bytes 1310720 | tf_op jit(solution)/shard_map/all_to_all | solution.py:317
  33.5 2.0 %collective-permute-start = (bf16[16,160,128]{2,1,0:T(8,128)(2,1)S(1)}, bf16[16,160,128]{2,1,0:T(8,128)(2,1)S(1)}, u32[]{:S(2)}, u32[]{:S(2)}) collective-permute-start(bf16[16,160,128]{2,1,0:T(8,128)(2,1)S(1)} %all_to_all.25.got_ref), channel_id=1, source_target_pairs={{0,1},{1,0},{2,3},{3,2},{4,5},{5,4},{6,7},{7,6},{8,9},{9,8},{10,11... | collective-permute-start | bytes 1966088 | tf_op jit(solution)/shard_map/ppermute | solution.py:325
  35.6 2.1 %collective-permute-done.other_ref = bf16[16,160,128]{2,1,0:T(8,128)(2,1)S(1)} collective-permute-done((bf16[16,160,128]{2,1,0:T(8,128)(2,1)S(1)}, bf16[16,160,128]{2,1,0:T(8,128)(2,1)S(1)}, u32[]{:S(2)}, u32[]{:S(2)}) %collective-permute-start) | collective-permute-done | bytes 655392 | tf_op jit(solution)/shard_map/ppermute | solution.py:325
  37.7 0.0 copy-done.2
  37.7 1.3 %shard_map.76 = f32[16,1,128]{2,1,0:T(1,128)} custom-call(bf16[16,160,128]{2,1,0:T(8,128)(2,1)S(1)} %all_to_all.25.got_ref, bf16[16,160,128]{2,1,0:T(8,128)(2,1)S(1)} %collective-permute-done.other_ref, f32[16,256]{1,0:T(8,128)S(1)} %copy-done.2, f32[1,16]{1,0:T(1,128)S(1)} %bitcast.3), custom_call_target="tpu_custom_call" | custom-call | flops 536870912 | tf_op jit(solution)/shard_map/pallas_call | solution.py:22
  39.0 3.6 %all-to-all-start.1 = ((f32[16,1,128]{2,1,0:T(1,128)}), f32[16,1,128]{2,1,0:T(1,128)S(1)}, u32[]{:S(2)}, u32[]{:S(2)}) async-start(f32[16,1,128]{2,1,0:T(1,128)} %shard_map.76), calls=%async_computation.1 | async-start | bytes 16384 | tf_op jit(solution)/shard_map/all_to_all | solution.py:317
  42.6 3.9 %shard_map.77 = (f32[256,256]{1,0:T(8,128)S(1)}, bf16[2048,256]{1,0:T(8,128)(2,1)S(1)}, bf16[16,256,128]{2,1,0:T(8,128)(2,1)S(1)}) custom-call(bf16[16,160,128]{2,1,0:T(8,128)(2,1)S(1)} %all_to_all.25.got_ref, bf16[16,160,128]{2,1,0:T(8,128)(2,1)S(1)} %collective-permute-done.other_ref), custom_call_target="tpu_custom_call" | custom-call | flops 1073741824 | tf_op jit(solution)/shard_map/pallas_call | solution.py:22
  46.5 0.0 copy-start.4
  46.5 0.7 copy-done.4
  47.2 2.5 %all-to-all-done.1.scores_ref = f32[16,1,128]{2,1,0:T(1,128)S(1)} async-done(((f32[16,1,128]{2,1,0:T(1,128)}), f32[16,1,128]{2,1,0:T(1,128)S(1)}, u32[]{:S(2)}, u32[]{:S(2)}) %all-to-all-start.1) | async-done | bytes 8224 | tf_op jit(solution)/shard_map/all_to_all | solution.py:317
  49.7 18.9 %all_to_all.26.pairs_ref = f32[32,2,128]{2,1,0:T(2,128)S(1)} all-to-all(f32[32,2,128]{2,1,0:T(2,128)S(1)} %shard_map.78), channel_id=1, replica_groups=mesh['dp'=16,'comp'=32] {'comp'}, dimensions={0} | all-to-all | bytes 65536 | tf_op jit(solution)/shard_map/all_to_all | solution.py:317
  68.6 0.6 shard_map.79
  69.1 13.8 %all_to_all.27.shares_ref = f32[16,16,128]{2,1,0:T(8,128)S(1)} all-to-all(f32[16,16,128]{2,1,0:T(8,128)S(1)} %get-tuple-element.25), channel_id=1, replica_groups=mesh['dp'=16,'comp'=32] {'dp'}, dimensions={0} | all-to-all | bytes 262144 | tf_op jit(solution)/shard_map/all_to_all | solution.py:317
  82.9 0.0 copy-done.5
  82.9 8.4 %shard_map.80 = f32[16,16,256]{2,1,0:T(8,128)} custom-call(f32[16,16,128]{2,1,0:T(8,128)S(1)} %all_to_all.27.shares_ref, bf16[2048,256]{1,0:T(8,128)(2,1)S(1)} %get-tuple-element.26.plain_ref, bf16[16,256,128]{2,1,0:T(8,128)(2,1)S(1)} %get-tuple-element.27.turned_ref, f32[256,256]{1,0:T(8,128)S(1)} %copy-done.5, f32[16,256]{1,0:T(8,128)S(1)} %copy-done.2, ...), custom_call_target="tpu_custom_call" | custom-call | flops 4294967296 | tf_op jit(solution)/shard_map/pallas_call | solution.py:22
  91.3 4.4 %all-to-all-start.4 = ((f32[16,16,256]{2,1,0:T(8,128)}), f32[16,16,256]{2,1,0:T(8,128)S(1)}, u32[]{:S(2)}, u32[]{:S(2)}) async-start(f32[16,16,256]{2,1,0:T(8,128)} %shard_map.80), calls=%async_computation.4 | async-start | bytes 524288 | tf_op jit(solution)/shard_map/all_to_all | solution.py:317
  95.7 1.1 %shard_map.81 = (f32[16,256]{1,0:T(8,128)}, f32[1,16]{1,0:T(1,128)}) custom-call(f32[16,16,128]{2,1,0:T(8,128)S(1)} %all_to_all.27.shares_ref, bf16[2048,256]{1,0:T(8,128)(2,1)S(1)} %get-tuple-element.26.plain_ref, f32[16,256]{1,0:T(8,128)S(1)} %copy-done.2, f32[1,16]{1,0:T(1,128)S(1)} %bitcast.5), custom_call_target="tpu_custom_call" | custom-call | flops 268435456 | tf_op jit(solution)/shard_map/pallas_call | solution.py:22
  96.9 8.7 %all-to-all-done.4 = f32[16,16,256]{2,1,0:T(8,128)S(1)} async-done(((f32[16,16,256]{2,1,0:T(8,128)}), f32[16,16,256]{2,1,0:T(8,128)S(1)}, u32[]{:S(2)}, u32[]{:S(2)}) %all-to-all-start.4) | async-done | bytes 262176 | tf_op jit(solution)/shard_map/all_to_all | solution.py:317
  105.6 0.7 copy.9
  (5 shorter events, 0.0 us)
Async XLA Ops:
  0.6 0.9 copy-start
  1.5 0.8 copy-start.1
  2.5 35.2 %copy-start.2 = (f32[16,256]{1,0:T(8,128)S(1)}, f32[16,256]{1,0:T(8,128)}, u32[]{:S(2)}) copy-start(f32[16,256]{1,0:T(8,128)} %centers_ref.5) | copy-start | bytes 49156
  33.5 4.1 %copy-start.3 = (f32[16]{0:T(128)S(1)}, f32[16]{0:T(128)}, u32[]{:S(2)}) copy-start(f32[16]{0:T(128)} %param.7) | copy-start | bytes 196
  33.5 4.1 %collective-permute-start = (bf16[16,160,128]{2,1,0:T(8,128)(2,1)S(1)}, bf16[16,160,128]{2,1,0:T(8,128)(2,1)S(1)}, u32[]{:S(2)}, u32[]{:S(2)}) collective-permute-start(bf16[16,160,128]{2,1,0:T(8,128)(2,1)S(1)} %all_to_all.25.got_ref), channel_id=1, source_target_pairs={{0,1},{1,0},{2,3},{3,2},{4,5},{5,4},{6,7},{7,6},{8,9},{9,8},{10,11... | collective-permute-start | bytes 1966088 | tf_op jit(solution)/shard_map/ppermute | solution.py:325
  39.0 10.7 %all-to-all-start.1 = ((f32[16,1,128]{2,1,0:T(1,128)}), f32[16,1,128]{2,1,0:T(1,128)S(1)}, u32[]{:S(2)}, u32[]{:S(2)}) async-start(f32[16,1,128]{2,1,0:T(1,128)} %shard_map.76), calls=%async_computation.1 | async-start | bytes 16384 | tf_op jit(solution)/shard_map/all_to_all | solution.py:317
  46.5 0.7 copy-start.4
  49.7 33.2 %copy-start.5 = (f32[256,256]{1,0:T(8,128)S(1)}, f32[256,256]{1,0:T(8,128)}, u32[]{:S(2)}) copy-start(f32[256,256]{1,0:T(8,128)} %copy-done.4) | copy-start | bytes 786436
  91.3 14.2 %all-to-all-start.4 = ((f32[16,16,256]{2,1,0:T(8,128)}), f32[16,16,256]{2,1,0:T(8,128)S(1)}, u32[]{:S(2)}, u32[]{:S(2)}) async-start(f32[16,16,256]{2,1,0:T(8,128)} %shard_map.80), calls=%async_computation.4 | async-start | bytes 524288 | tf_op jit(solution)/shard_map/all_to_all | solution.py:317

commit v3 on v2

v3 whole, which is shorter than its diff:
```python
import jax
import jax.numpy as jnp
from jax import lax
from jax.experimental import pallas as pl
from jax.experimental.pallas import tpu as pltpu
from jax.sharding import PartitionSpec as P

step_weight = 0.5
ridge_term = 0.01
normal_offset = 0.9189385332046727
exact_mode = lax.Precision.HIGHEST
PANEL = 32
SUB = 16
SQUARE, BOTH, START, TABLES = 0, 2, 4, 6
f32 = jnp.float32
bf16 = jnp.bfloat16


def call(body, out_shape, *args, scratch=(), flops=0, near=True):
    single = not isinstance(out_shape, (list, tuple))
    vmem = pl.BlockSpec(memory_space=pltpu.VMEM)
    space = pltpu.VMEM if near else pltpu.HBM
    args = [pltpu.with_memory_space_constraint(arg, space) for arg in args]
    return pl.pallas_call(
        body,
        out_shape=out_shape,
        in_specs=[vmem] * len(args),
        out_specs=vmem if single else [vmem] * len(out_shape),
        scratch_shapes=list(scratch),
        cost_estimate=pl.CostEstimate(flops=flops, transcendentals=0, bytes_accessed=0),
        compiler_params=pltpu.CompilerParams(vmem_limit_bytes=12 << 20),
    )(*args)


def place():
    return lax.axis_index("dp"), lax.axis_index("comp") % 2


def shape(dims, dtype=f32):
    return pltpu.VMEM(dims, dtype)


def far(dims, dtype=f32):
    return jax.ShapeDtypeStruct(dims, dtype)


def own_of(row_ref, position):
    row = row_ref[...]
    lanes = lax.broadcasted_iota(jnp.int32, row.shape, 1)
    return jnp.sum(jnp.where(lanes == position, row, 0.0), axis=1, keepdims=True)


def eye_of(size):
    rows = lax.broadcasted_iota(jnp.int32, (size, size), 0)
    cols = lax.broadcasted_iota(jnp.int32, (size, size), 1)
    return rows, cols


def three_parts(wide):
    high = wide.astype(bf16)
    rest = wide - high.astype(f32)
    mid = rest.astype(bf16)
    low = (rest - mid.astype(f32)).astype(bf16)
    return high, mid, low


def over_lanes(left, right):
    return lax.dot_general(left, right, (((1,), (1,)), ((), ())), preferred_element_type=f32)


def spread_body(vectors_ref, factors_ref, out_ref):
    unused, core = place()
    half = vectors_ref[:, pl.ds(pl.multiple_of(core * 128, 128), 128)]
    for peer in range(out_ref.shape[0]):
        out_ref[peer, :128, :] = half
        out_ref[peer, 128:144, :] = factors_ref[peer, :, :128]
        out_ref[peer, 144:160, :] = factors_ref[peer, :, 128:]


def gather_factor(got_ref, factor_ref):
    for peer in range(16):
        factor_ref[16 * peer : 16 * peer + 16, :128] = got_ref[peer, 128:144, :]
        factor_ref[16 * peer : 16 * peer + 16, 128:] = got_ref[peer, 144:160, :]


def score_body(got_ref, other_ref, centers_ref, mixing_ref, out_ref, factor_ref):
    position, core = place()
    gather_factor(got_ref, factor_ref)
    wide = factor_ref[...].astype(f32)
    center = centers_ref[pl.ds(position, 1), :]
    shifted = jnp.sum(wide * center, axis=1, keepdims=True)
    rows, cols = eye_of(256)
    diagonal = jnp.sum(jnp.where(rows == cols, wide, 0.0), axis=1, keepdims=True)
    log_diag = jnp.sum(jnp.log(diagonal), axis=0, keepdims=True)
    log_mix = jnp.log(own_of(mixing_ref, position))
    mine = factor_ref[:, pl.ds(pl.multiple_of(core * 128, 128), 128)]
    rest = factor_ref[:, pl.ds(pl.multiple_of((1 - core) * 128, 128), 128)]
    for pair in range(8):
        ours = got_ref[2 * pair : 2 * pair + 2, :128, :].reshape(256, 128)
        theirs = other_ref[2 * pair : 2 * pair + 2, :128, :].reshape(256, 128)
        whitened = over_lanes(mine, ours) + over_lanes(rest, theirs)
        whitened -= shifted
        density = log_diag - 0.5 * jnp.sum(whitened * whitened, axis=0, keepdims=True)
        scores = density + log_mix - 256 * normal_offset
        out_ref[2 * pair] = scores[:, :128]
        out_ref[2 * pair + 1] = scores[:, 128:]


def apart(left, right, **options):
    return jnp.dot(left, right, precision=exact_mode, preferred_element_type=f32)


def invert_body(got_ref, tables_ref, factor_ref, inverse_ref):
    gather_factor(got_ref, factor_ref)
    rows, cols = eye_of(128)
    factors = []
    for start in (0, 128):
        factor = factor_ref[start : start + 128, start : start + 128].astype(f32)
        diagonal = jnp.sum(jnp.where(rows == cols, factor, 0.0), axis=1, keepdims=True)
        factors.append(factor)
        inverse_ref[start // 128] = jnp.where(rows == cols, 1.0 / diagonal, 0.0)
    for level in range(7):
        below = (rows >> (level + 1) == cols >> (level + 1)) & (rows >> level > cols >> level)
        for block in range(2):
            inverse = inverse_ref[block]
            step = jnp.where(below, factors[block], 0.0)
            inverse_ref[block] = inverse - apart(apart(inverse, step), inverse)
    first, last = inverse_ref[0], inverse_ref[1]
    corner = -apart(apart(last, factor_ref[128:, :128].astype(f32)), first)
    bottom = jnp.concatenate([corner, last], axis=1)
    whole = jnp.concatenate(
        [jnp.concatenate([first, jnp.zeros((128, 128), f32)], axis=1), bottom], axis=0
    )
    square = lax.dot_general(
        whole, whole, (((1,), (1,)), ((), ())), precision=exact_mode, preferred_element_type=f32
    )
    rows, cols = eye_of(256)
    diagonal = jnp.where(rows == cols, square, 0.0)
    down = lax.rsqrt(1.0 + jnp.sum(diagonal, axis=1, keepdims=True))
    across = lax.rsqrt(1.0 + jnp.sum(diagonal, axis=0, keepdims=True))
    both = down * across
    tables = (square * both, both, jnp.where(rows == cols, across, 0.0))
    for place, table in zip((SQUARE, BOTH, START), tables):
        tables_ref[place] = table[:, :128]
        tables_ref[place + 1] = table[:, 128:]


INV_SCRATCH = [pltpu.VMEM((256, 256), bf16), pltpu.VMEM((2, 128, 128), f32)]


def order_body(got_ref, other_ref, turned_ref):
    unused, core = place()
    ours = pl.ds(pl.multiple_of(core * 128, 128), 128)
    theirs = pl.ds(pl.multiple_of((1 - core) * 128, 128), 128)
    for block in range(16):
        turned_ref[block, ours, :] = got_ref[block, :128, :].T
        turned_ref[block, theirs, :] = other_ref[block, :128, :].T


def prepare_body(got_ref, other_ref, tables_ref, turned_ref, factor_ref, inverse_ref):
    invert_body(got_ref, tables_ref, factor_ref, inverse_ref)
    order_body(got_ref, other_ref, turned_ref)


def partial_body(scores_ref, out_ref):
    scores = scores_ref[:, 0, :]
    top = jnp.max(scores, axis=0, keepdims=True)
    total = jnp.sum(jnp.exp(scores - top), axis=0, keepdims=True)
    both = jnp.concatenate([top, total], axis=0)
    for peer in range(out_ref.shape[0]):
        out_ref[peer] = both


def share_body(scores_ref, pairs_ref, shares_ref, evidence_ref):
    tops, totals = pairs_ref[:, 0, :], pairs_ref[:, 1, :]
    top = jnp.max(tops, axis=0, keepdims=True)
    total = jnp.sum(totals * jnp.exp(tops - top), axis=0, keepdims=True)
    evidence_ref[...] = top + jnp.log(total)
    shares = jnp.exp(scores_ref[:, 0, :] - top) / total
    for peer in range(shares_ref.shape[0]):
        shares_ref[peer] = shares


def same_row(tile, row):
    return jnp.broadcast_to(tile[row : row + 1, :], tile.shape)


def eliminate(work_ref, tables_ref, out_ref):
    size, panel, sub = 256, PANEL, SUB
    tiles = panel // 8
    in_tile = lax.broadcasted_iota(jnp.int32, (8, 128), 0)
    lane_of = lax.broadcasted_iota(jnp.int32, (8, 128), 1)
    far_lane = lax.broadcasted_iota(jnp.int32, (1, 128), 1)
    for start in range(0, size, panel):
        stop = start + panel
        near = start // 128
        rows = [
            [work_ref[start + 8 * i : start + 8 * i + 8, 128 * t : 128 * t + 128] for i in range(tiles)]
            for t in range(2)
        ]
        scale = [jnp.zeros((8, 128), f32) for i in range(tiles)]
        for begin in range(0, panel, sub):
            lane = start % 128 + begin
            columns = [
                {
                    i: jnp.broadcast_to(rows[near][i][:, lane + k : lane + k + 1], (8, 128))
                    for i in range((begin + k) // 8, tiles)
                }
                for k in range(sub)
            ]
            cleared = (lane_of >= lane) & (lane_of < lane + sub)
            for i in range(tiles):
                fresh = tables_ref[START + near, start + 8 * i : start + 8 * i + 8, :]
                rows[near][i] = jnp.where(cleared, fresh, rows[near][i])
            for k in range(0, sub, 2):
                row = begin + k
                tile, place = row // 8, row % 8
                one, two = columns[k], columns[k + 1]
                a, b = same_row(one[tile], place), same_row(one[tile], place + 1)
                d = same_row(two[tile], place + 1)
                root = lax.rsqrt(a * d - b * b)
                inverse = root * root
                root_a = lax.rsqrt(a)
                raw = {
                    i: (one[i] * d - two[i] * b, two[i] * a - one[i] * b)
                    for i in range(tile, tiles)
                }
                below = in_tile > place + 1
                raw[tile] = tuple(jnp.where(below, part, 0.0) for part in raw[tile])
                ratio = {i: (raw[i][0] * inverse, raw[i][1] * inverse) for i in raw}
                for later in range(k + 2, sub):
                    other = begin + later
                    f = same_row(one[other // 8], other % 8)
                    g = same_row(two[other // 8], other % 8)
                    for i in range(other // 8, tiles):
                        if later < k + 4:
                            change = (raw[i][0] * f + raw[i][1] * g) * inverse
                        else:
                            change = ratio[i][0] * f + ratio[i][1] * g
                        columns[later][i] = columns[later][i] - change
                ratio[tile] = (
                    jnp.where(in_tile == place + 1, b * (root_a * root_a), ratio[tile][0]),
                    ratio[tile][1],
                )
                for group in rows:
                    f, g = same_row(group[tile], place), same_row(group[tile], place + 1)
                    for i in range(tile, tiles):
                        group[i] = group[i] - (ratio[i][0] * f + ratio[i][1] * g)
                scale[tile] = jnp.where(in_tile == place, root_a, scale[tile])
                scale[tile] = jnp.where(in_tile == place + 1, root * (a * root_a), scale[tile])
        solved = [
            jnp.concatenate([group[i] * scale[i] for i in range(tiles)], axis=0) for group in rows
        ]
        for t in range(2):
            lanes = slice(128 * t, 128 * t + 128)
            done = jnp.where(far_lane + 128 * t < stop, solved[t], 0.0)
            for piece in range(panel // 16):
                out_ref[start // 16 + piece, :, lanes] = done[16 * piece : 16 * piece + 16, :]
        if stop == size:
            break
        high, mid, low = three_parts(jnp.concatenate(solved, axis=1))
        straight = jnp.concatenate([high, mid, high, low, high, mid], axis=0)
        turned = jnp.concatenate([high, high, mid, high, low, mid], axis=0)
        inside = (far_lane + 128 * near >= start) & (far_lane + 128 * near < stop)
        for mine in range(stop // 128, 2):
            change = lax.dot_general(
                turned[:, 128 * mine : 128 * mine + 128],
                straight,
                (((0,), (0,)), ((), ())),
                preferred_element_type=f32,
            )
            begin = max(stop, 128 * mine)
            skip = begin - 128 * mine
            for t in range(2):
                lanes = slice(128 * t, 128 * t + 128)
                kept = work_ref[begin : 128 * mine + 128, lanes]
                if t == near:
                    kept = jnp.where(inside, 0.0, kept)
                work_ref[begin : 128 * mine + 128, lanes] = kept - change[skip:, lanes]


def refactor_body(
    shares_ref, turned_ref, tables_ref, centers_ref, mixing_ref, out_ref, work_ref
):
    position, unused = place()
    vector_total = turned_ref.shape[0] * turned_ref.shape[2]
    share = shares_ref[:, pl.ds(position, 1), :].reshape(16, 128)
    gram = jnp.zeros((256, 256), f32)
    moment = jnp.zeros((256, 128), f32)
    for pair in range(8):
        weighted = []
        for block in (2 * pair, 2 * pair + 1):
            weighted.append(turned_ref[block].astype(f32) * share[block : block + 1, :])
            moment += weighted[-1]
        vectors = jnp.concatenate([turned_ref[2 * pair], turned_ref[2 * pair + 1]], axis=1)
        for part in three_parts(jnp.concatenate(weighted, axis=1)):
            gram += over_lanes(part, vectors)
    counts = jnp.sum(jnp.sum(share, axis=1, keepdims=True), axis=0, keepdims=True)
    moment = jnp.sum(moment, axis=1, keepdims=True)
    rows, cols = eye_of(256)
    same = rows == cols
    prior = own_of(mixing_ref, position)
    kept = (1.0 - step_weight) * prior
    weight = kept + step_weight * counts / vector_total
    center = centers_ref[pl.ds(position, 1), :]
    center_down = jnp.sum(jnp.where(same, center, 0.0), axis=1, keepdims=True)
    mean_down = (kept * center_down + step_weight * moment / vector_total) / weight
    mean = jnp.sum(jnp.where(same, mean_down, 0.0), axis=0, keepdims=True)
    moment_part = (
        ((kept * center_down) * center + (step_weight / vector_total) * gram) / weight
        - mean_down * mean
        + jnp.where(same, ridge_term, 0.0)
    )
    for t in range(2):
        lanes = slice(128 * t, 128 * t + 128)
        work_ref[:, lanes] = (kept / weight) * tables_ref[SQUARE + t] + moment_part[:, lanes] * (
            tables_ref[BOTH + t]
        )
    eliminate(work_ref, tables_ref, out_ref)


def means_body(shares_ref, turned_ref, centers_ref, mixing_ref, means_ref, weights_ref):
    vector_total = turned_ref.shape[0] * turned_ref.shape[2]
    moment = jnp.zeros((16, 256), f32)
    counts = jnp.zeros((16, 128), f32)
    for block in range(16):
        share = shares_ref[block]
        counts += share
        for part in three_parts(share):
            moment += over_lanes(part, turned_ref[block])
    counts = jnp.sum(counts, axis=1, keepdims=True)
    rows, cols = eye_of(16)
    prior = jnp.sum(jnp.where(rows == cols, mixing_ref[...], 0.0), axis=1, keepdims=True)
    kept = (1.0 - step_weight) * prior
    weights = kept + step_weight * counts / vector_total
    weights_ref[...] = jnp.sum(jnp.where(rows == cols, weights, 0.0), axis=0, keepdims=True)
    means_ref[...] = (
        kept * centers_ref[...] + step_weight * moment / vector_total
    ) / weights


def exchanged(array, axis):
    return lax.all_to_all(array, axis, split_axis=0, concat_axis=0, tiled=True)


def local(vectors, centers, factors, mixing):
    groups, peers = lax.axis_size("dp"), lax.axis_size("comp")
    priors = mixing.reshape(1, 16)
    spread = call(spread_body, shape((groups, 160, 128), bf16), vectors, factors, near=False)
    got = exchanged(spread, "dp")
    other = lax.ppermute(got, "comp", [(i, i ^ 1) for i in range(peers)])
    scores = call(
        score_body, shape((16, 1, 128)), got, other, centers, priors,
        scratch=[pltpu.VMEM((256, 256), bf16)], flops=1 << 29,
    )
    scores, after, after_other = lax.optimization_barrier((scores, got, other))
    scores_here = exchanged(scores, "dp")
    tables, turned = call(
        prepare_body,
        [shape((TABLES, 256, 128)), shape((16, 256, 128), bf16)],
        after, after_other, scratch=INV_SCRATCH, flops=1 << 30,
    )
    scores_here, tables, turned = lax.optimization_barrier((scores_here, tables, turned))
    partial = call(partial_body, shape((peers, 2, 128)), scores_here)
    pairs = exchanged(partial, "comp")
    shares, evidence = call(
        share_body, [shape((groups, 16, 128)), far((1, 128))], scores_here, pairs
    )
    shares_all = exchanged(shares, "dp")
    refreshed = call(
        refactor_body, shape((16, 16, 256)), shares_all, turned, tables, centers,
        priors, scratch=[pltpu.VMEM((256, 256), f32)], flops=1 << 32,
    )
    new_factors = exchanged(refreshed, "dp")
    new_means, new_weights = call(
        means_body, [far((16, 256)), far((1, 16))], shares_all, turned, centers, priors,
        flops=1 << 28,
    )
    return new_factors, new_means, new_weights.reshape(16), evidence.reshape(128)


def solution(mesh):
    return jax.shard_map(
        local,
        mesh=mesh,
        in_specs=(P("dp", None), P("comp", None), P("comp", "dp", None), P("comp")),
        out_specs=(P("comp", "dp", None), P("comp", None), P("comp"), P("dp")),
        check_vma=False,
    )
```

time: 107 us -> 105 us (0.981)
  local copies, waits for them, and re-layouts: 3.15 us -> 0.71 us
    unnamed x13 -> x5, local copies, waits for them, and re-layouts: 3.15 us -> 0.71 us
where the time goes in v3:
time: 105 us; the launch traced here: 104 us
  blocking collectives  62.9 us (60%)
  Pallas kernels  16.3 us (16%)
  waiting for transfers between devices  13.5 us (13%)
  starting transfers between devices  10 us (10%)
    all_to_all x3, blocking collectives, exchanged(): return lax.all_to_all(array, axis, split_axis=0, concat_axis=0, tiled=True)  62.9 us
    pallas_call x7, Pallas kernels, call(): pl.pallas_call(body, out_shape=out_shape, in_specs=[vmem] * len(args), ou...  16.3 us
    all_to_all x2, waiting for transfers between devices, exchanged(): return lax.all_to_all(array, axis, split_axis=0, concat_axis=0, tiled=True)  11.4 us
    all_to_all x2, starting transfers between devices, exchanged(): return lax.all_to_all(array, axis, split_axis=0, concat_axis=0, tiled=True)  7.97 us
  transfers between devices with their start and end apart: 3, of which 3 were waited for; matrix products, arithmetic and copies ran while one was open for 0% of the time, Pallas kernels for 5%

profile of v3, /device:TPU:8, one launch (start us, length us, event | category | flops | bytes accessed | tf_op | source)
XLA Modules:
  0.0 104.1 jit_solution(9141078645129542161)
XLA Ops:
  0.6 1.0 shard_map.75
  1.7 0.0 copy-start
  1.7 31.1 %all_to_all.25.got_ref = bf16[16,160,128]{2,1,0:T(8,128)(2,1)S(1)} all-to-all(bf16[16,160,128]{2,1,0:T(8,128)(2,1)S(1)} %shard_map.75), channel_id=1, replica_groups=mesh['dp'=16,'comp'=32] {'dp'}, dimensions={0} | all-to-all | bytes 1310720 | tf_op jit(solution)/shard_map/all_to_all | solution.py:343
  32.7 0.0 copy-start.1
  32.7 2.0 %collective-permute-start = (bf16[16,160,128]{2,1,0:T(8,128)(2,1)S(1)}, bf16[16,160,128]{2,1,0:T(8,128)(2,1)S(1)}, u32[]{:S(2)}, u32[]{:S(2)}) collective-permute-start(bf16[16,160,128]{2,1,0:T(8,128)(2,1)S(1)} %all_to_all.25.got_ref), channel_id=1, source_target_pairs={{0,1},{1,0},{2,3},{3,2},{4,5},{5,4},{6,7},{7,6},{8,9},{9,8},{10,11... | collective-permute-start | bytes 1966088 | tf_op jit(solution)/shard_map/ppermute | solution.py:351
  34.8 2.1 %collective-permute-done.other_ref = bf16[16,160,128]{2,1,0:T(8,128)(2,1)S(1)} collective-permute-done((bf16[16,160,128]{2,1,0:T(8,128)(2,1)S(1)}, bf16[16,160,128]{2,1,0:T(8,128)(2,1)S(1)}, u32[]{:S(2)}, u32[]{:S(2)}) %collective-permute-start) | collective-permute-done | bytes 655392 | tf_op jit(solution)/shard_map/ppermute | solution.py:351
  36.9 0.0 copy-done
  36.9 0.0 copy-done.1
  36.9 1.3 %shard_map.76 = f32[16,1,128]{2,1,0:T(1,128)} custom-call(bf16[16,160,128]{2,1,0:T(8,128)(2,1)S(1)} %all_to_all.25.got_ref, bf16[16,160,128]{2,1,0:T(8,128)(2,1)S(1)} %collective-permute-done.other_ref, f32[16,256]{1,0:T(8,128)S(1)} %copy-done, f32[1,16]{1,0:T(1,128)S(1)} %bitcast.3), custom_call_target="tpu_custom_call" | custom-call | flops 536870912 | tf_op jit(solution)/shard_map/pallas_call | solution.py:24
  38.2 3.6 %all-to-all-start.1 = ((f32[16,1,128]{2,1,0:T(1,128)}), f32[16,1,128]{2,1,0:T(1,128)S(1)}, u32[]{:S(2)}, u32[]{:S(2)}) async-start(f32[16,1,128]{2,1,0:T(1,128)} %shard_map.76), calls=%async_computation.1 | async-start | bytes 16384 | tf_op jit(solution)/shard_map/all_to_all | solution.py:343
  41.8 4.0 %shard_map.77 = (f32[6,256,128]{2,1,0:T(8,128)S(1)}, bf16[16,256,128]{2,1,0:T(8,128)(2,1)S(1)}) custom-call(bf16[16,160,128]{2,1,0:T(8,128)(2,1)S(1)} %all_to_all.25.got_ref, bf16[16,160,128]{2,1,0:T(8,128)(2,1)S(1)} %collective-permute-done.other_ref), custom_call_target="tpu_custom_call" | custom-call | flops 1073741824 | tf_op jit(solution)/shard_map/pallas_call | solution.py:24
  45.7 3.1 %all-to-all-done.1.scores_ref = f32[16,1,128]{2,1,0:T(1,128)S(1)} async-done(((f32[16,1,128]{2,1,0:T(1,128)}), f32[16,1,128]{2,1,0:T(1,128)S(1)}, u32[]{:S(2)}, u32[]{:S(2)}) %all-to-all-start.1) | async-done | bytes 8224 | tf_op jit(solution)/shard_map/all_to_all | solution.py:343
  48.9 18.7 %all_to_all.26.pairs_ref = f32[32,2,128]{2,1,0:T(2,128)S(1)} all-to-all(f32[32,2,128]{2,1,0:T(2,128)S(1)} %shard_map.78), channel_id=1, replica_groups=mesh['dp'=16,'comp'=32] {'comp'}, dimensions={0} | all-to-all | bytes 65536 | tf_op jit(solution)/shard_map/all_to_all | solution.py:343
  67.6 0.6 shard_map.79
  68.2 13.1 %all_to_all.27.shares_ref = f32[16,16,128]{2,1,0:T(8,128)S(1)} all-to-all(f32[16,16,128]{2,1,0:T(8,128)S(1)} %get-tuple-element.22), channel_id=1, replica_groups=mesh['dp'=16,'comp'=32] {'dp'}, dimensions={0} | all-to-all | bytes 262144 | tf_op jit(solution)/shard_map/all_to_all | solution.py:343
  81.3 7.9 %shard_map.80 = f32[16,16,256]{2,1,0:T(8,128)} custom-call(f32[16,16,128]{2,1,0:T(8,128)S(1)} %all_to_all.27.shares_ref, bf16[16,256,128]{2,1,0:T(8,128)(2,1)S(1)} %get-tuple-element.23.turned_ref, f32[6,256,128]{2,1,0:T(8,128)S(1)} %get-tuple-element.24.tables_ref, f32[16,256]{1,0:T(8,128)S(1)} %copy-done, f32[1,16]{1,0:T(1,128)S(1)} %bitcast.4), custom_call_target="tpu_custom_call" | custom-call | flops 4294967296 | tf_op jit(solution)/shard_map/pallas_call | solution.py:24
  89.2 4.4 %all-to-all-start.4 = ((f32[16,16,256]{2,1,0:T(8,128)}), f32[16,16,256]{2,1,0:T(8,128)S(1)}, u32[]{:S(2)}, u32[]{:S(2)}) async-start(f32[16,16,256]{2,1,0:T(8,128)} %shard_map.80), calls=%async_computation.4 | async-start | bytes 524288 | tf_op jit(solution)/shard_map/all_to_all | solution.py:343
  93.6 1.5 %shard_map.81 = (f32[16,256]{1,0:T(8,128)}, f32[1,16]{1,0:T(1,128)}) custom-call(f32[16,16,128]{2,1,0:T(8,128)S(1)} %all_to_all.27.shares_ref, bf16[16,256,128]{2,1,0:T(8,128)(2,1)S(1)} %get-tuple-element.23.turned_ref, f32[16,256]{1,0:T(8,128)S(1)} %copy-done, f32[1,16]{1,0:T(1,128)S(1)} %bitcast.5), custom_call_target="tpu_custom_call" | custom-call | flops 268435456 | tf_op jit(solution)/shard_map/pallas_call | solution.py:24
  95.1 8.3 %all-to-all-done.4 = f32[16,16,256]{2,1,0:T(8,128)S(1)} async-done(((f32[16,16,256]{2,1,0:T(8,128)}), f32[16,16,256]{2,1,0:T(8,128)S(1)}, u32[]{:S(2)}, u32[]{:S(2)}) %all-to-all-start.4) | async-done | bytes 262176 | tf_op jit(solution)/shard_map/all_to_all | solution.py:343
  103.4 0.7 copy.9
  (1 shorter events, 0.0 us)
Async XLA Ops:
  1.7 35.2 %copy-start = (f32[16,256]{1,0:T(8,128)S(1)}, f32[16,256]{1,0:T(8,128)}, u32[]{:S(2)}) copy-start(f32[16,256]{1,0:T(8,128)} %centers_ref.5) | copy-start | bytes 49156
  32.7 4.1 %copy-start.1 = (f32[16]{0:T(128)S(1)}, f32[16]{0:T(128)}, u32[]{:S(2)}) copy-start(f32[16]{0:T(128)} %param.7) | copy-start | bytes 196
  32.7 4.1 %collective-permute-start = (bf16[16,160,128]{2,1,0:T(8,128)(2,1)S(1)}, bf16[16,160,128]{2,1,0:T(8,128)(2,1)S(1)}, u32[]{:S(2)}, u32[]{:S(2)}) collective-permute-start(bf16[16,160,128]{2,1,0:T(8,128)(2,1)S(1)} %all_to_all.25.got_ref), channel_id=1, source_target_pairs={{0,1},{1,0},{2,3},{3,2},{4,5},{5,4},{6,7},{7,6},{8,9},{9,8},{10,11... | collective-permute-start | bytes 1966088 | tf_op jit(solution)/shard_map/ppermute | solution.py:351
  38.2 10.7 %all-to-all-start.1 = ((f32[16,1,128]{2,1,0:T(1,128)}), f32[16,1,128]{2,1,0:T(1,128)S(1)}, u32[]{:S(2)}, u32[]{:S(2)}) async-start(f32[16,1,128]{2,1,0:T(1,128)} %shard_map.76), calls=%async_computation.1 | async-start | bytes 16384 | tf_op jit(solution)/shard_map/all_to_all | solution.py:343
  89.2 14.2 %all-to-all-start.4 = ((f32[16,16,256]{2,1,0:T(8,128)}), f32[16,16,256]{2,1,0:T(8,128)S(1)}, u32[]{:S(2)}, u32[]{:S(2)}) async-start(f32[16,16,256]{2,1,0:T(8,128)} %shard_map.80), calls=%async_computation.4 | async-start | bytes 524288 | tf_op jit(solution)/shard_map/all_to_all | solution.py:343

commit v4 on v3

v4 whole, which is shorter than its diff:
```python
import jax
import jax.numpy as jnp
from jax import lax
from jax.experimental import pallas as pl
from jax.experimental.pallas import tpu as pltpu
from jax.sharding import PartitionSpec as P

step_weight = 0.5
ridge_term = 0.01
normal_offset = 0.9189385332046727
exact_mode = lax.Precision.HIGHEST
PANEL = 32
SUB = 16
SQUARE, BOTH, START, TABLES = 0, 2, 4, 6
f32 = jnp.float32
bf16 = jnp.bfloat16


def call(body, out_shape, *args, scratch=(), flops=0, near=True):
    single = not isinstance(out_shape, (list, tuple))
    vmem = pl.BlockSpec(memory_space=pltpu.VMEM)
    hbm = pl.BlockSpec(memory_space=pltpu.HBM)
    space = pltpu.VMEM if near else pltpu.HBM
    args = [pltpu.with_memory_space_constraint(arg, space) for arg in args]
    return pl.pallas_call(
        body,
        out_shape=out_shape,
        in_specs=[vmem] * len(args),
        out_specs=vmem if single else [
            hbm if out.memory_space == pltpu.HBM else vmem for out in out_shape
        ],
        scratch_shapes=list(scratch),
        cost_estimate=pl.CostEstimate(flops=flops, transcendentals=0, bytes_accessed=0),
        compiler_params=pltpu.CompilerParams(vmem_limit_bytes=12 << 20),
    )(*args)


def place():
    return lax.axis_index("dp"), lax.axis_index("comp") % 2


def shape(dims, dtype=f32):
    return pltpu.VMEM(dims, dtype)


def far(dims, dtype=f32):
    return pltpu.HBM(dims, dtype)


def own_of(row_ref, position):
    row = row_ref[...]
    lanes = lax.broadcasted_iota(jnp.int32, row.shape, 1)
    return jnp.sum(jnp.where(lanes == position, row, 0.0), axis=1, keepdims=True)


def eye_of(size):
    rows = lax.broadcasted_iota(jnp.int32, (size, size), 0)
    cols = lax.broadcasted_iota(jnp.int32, (size, size), 1)
    return rows, cols


def three_parts(wide):
    high = wide.astype(bf16)
    rest = wide - high.astype(f32)
    mid = rest.astype(bf16)
    low = (rest - mid.astype(f32)).astype(bf16)
    return high, mid, low


def over_lanes(left, right):
    return lax.dot_general(left, right, (((1,), (1,)), ((), ())), preferred_element_type=f32)


def spread_body(vectors_ref, factors_ref, out_ref):
    unused, core = place()
    half = vectors_ref[:, pl.ds(pl.multiple_of(core * 128, 128), 128)]
    for peer in range(out_ref.shape[0]):
        out_ref[peer, :128, :] = half
        out_ref[peer, 128:144, :] = factors_ref[peer, :, :128]
        out_ref[peer, 144:160, :] = factors_ref[peer, :, 128:]


def gather_factor(got_ref, factor_ref):
    for peer in range(16):
        factor_ref[16 * peer : 16 * peer + 16, :128] = got_ref[peer, 128:144, :]
        factor_ref[16 * peer : 16 * peer + 16, 128:] = got_ref[peer, 144:160, :]


def score_body(got_ref, other_ref, centers_ref, mixing_ref, out_ref, factor_ref):
    position, core = place()
    gather_factor(got_ref, factor_ref)
    wide = factor_ref[...].astype(f32)
    center = centers_ref[pl.ds(position, 1), :]
    shifted = jnp.sum(wide * center, axis=1, keepdims=True)
    rows, cols = eye_of(256)
    diagonal = jnp.sum(jnp.where(rows == cols, wide, 0.0), axis=1, keepdims=True)
    log_diag = jnp.sum(jnp.log(diagonal), axis=0, keepdims=True)
    log_mix = jnp.log(own_of(mixing_ref, position))
    mine = factor_ref[:, pl.ds(pl.multiple_of(core * 128, 128), 128)]
    rest = factor_ref[:, pl.ds(pl.multiple_of((1 - core) * 128, 128), 128)]
    for pair in range(8):
        ours = got_ref[2 * pair : 2 * pair + 2, :128, :].reshape(256, 128)
        theirs = other_ref[2 * pair : 2 * pair + 2, :128, :].reshape(256, 128)
        whitened = over_lanes(mine, ours) + over_lanes(rest, theirs)
        whitened -= shifted
        density = log_diag - 0.5 * jnp.sum(whitened * whitened, axis=0, keepdims=True)
        scores = density + log_mix - 256 * normal_offset
        out_ref[2 * pair] = scores[:, :128]
        out_ref[2 * pair + 1] = scores[:, 128:]


def apart(left, right, **options):
    return jnp.dot(left, right, precision=exact_mode, preferred_element_type=f32)


def invert_body(got_ref, tables_ref, factor_ref, inverse_ref):
    gather_factor(got_ref, factor_ref)
    rows, cols = eye_of(128)
    factors = []
    for start in (0, 128):
        factor = factor_ref[start : start + 128, start : start + 128].astype(f32)
        diagonal = jnp.sum(jnp.where(rows == cols, factor, 0.0), axis=1, keepdims=True)
        factors.append(factor)
        inverse_ref[start // 128] = jnp.where(rows == cols, 1.0 / diagonal, 0.0)
    for level in range(7):
        below = (rows >> (level + 1) == cols >> (level + 1)) & (rows >> level > cols >> level)
        for block in range(2):
            inverse = inverse_ref[block]
            step = jnp.where(below, factors[block], 0.0)
            inverse_ref[block] = inverse - apart(apart(inverse, step), inverse)
    first, last = inverse_ref[0], inverse_ref[1]
    corner = -apart(apart(last, factor_ref[128:, :128].astype(f32)), first)
    bottom = jnp.concatenate([corner, last], axis=1)
    whole = jnp.concatenate(
        [jnp.concatenate([first, jnp.zeros((128, 128), f32)], axis=1), bottom], axis=0
    )
    square = lax.dot_general(
        whole, whole, (((1,), (1,)), ((), ())), precision=exact_mode, preferred_element_type=f32
    )
    rows, cols = eye_of(256)
    diagonal = jnp.where(rows == cols, square, 0.0)
    down = lax.rsqrt(1.0 + jnp.sum(diagonal, axis=1, keepdims=True))
    across = lax.rsqrt(1.0 + jnp.sum(diagonal, axis=0, keepdims=True))
    both = down * across
    tables = (square * both, both, jnp.where(rows == cols, across, 0.0))
    for place, table in zip((SQUARE, BOTH, START), tables):
        tables_ref[place] = table[:, :128]
        tables_ref[place + 1] = table[:, 128:]


INV_SCRATCH = [pltpu.VMEM((256, 256), bf16), pltpu.VMEM((2, 128, 128), f32)]


def order_body(got_ref, other_ref, turned_ref):
    unused, core = place()
    ours = pl.ds(pl.multiple_of(core * 128, 128), 128)
    theirs = pl.ds(pl.multiple_of((1 - core) * 128, 128), 128)
    for block in range(16):
        turned_ref[block, ours, :] = got_ref[block, :128, :].T
        turned_ref[block, theirs, :] = other_ref[block, :128, :].T


def prepare_body(got_ref, other_ref, tables_ref, turned_ref, factor_ref, inverse_ref):
    invert_body(got_ref, tables_ref, factor_ref, inverse_ref)
    order_body(got_ref, other_ref, turned_ref)


def partial_body(scores_ref, out_ref):
    scores = scores_ref[:, 0, :]
    top = jnp.max(scores, axis=0, keepdims=True)
    total = jnp.sum(jnp.exp(scores - top), axis=0, keepdims=True)
    both = jnp.concatenate([top, total], axis=0)
    for peer in range(out_ref.shape[0]):
        out_ref[peer] = both


def share_body(scores_ref, pairs_ref, shares_ref, evidence_ref):
    tops, totals = pairs_ref[:, 0, :], pairs_ref[:, 1, :]
    top = jnp.max(tops, axis=0, keepdims=True)
    total = jnp.sum(totals * jnp.exp(tops - top), axis=0, keepdims=True)
    evidence_ref[...] = top + jnp.log(total)
    shares = jnp.exp(scores_ref[:, 0, :] - top) / total
    for peer in range(shares_ref.shape[0]):
        shares_ref[peer] = shares


def same_row(tile, row):
    return jnp.broadcast_to(tile[row : row + 1, :], tile.shape)


def six_products(rows):
    high, mid, low = three_parts(rows)
    turned = jnp.concatenate([high, high, mid, high, low, mid], axis=0)
    straight = jnp.concatenate([high, mid, high, low, high, mid], axis=0)
    return turned, straight


def over_rows(left, right):
    return lax.dot_general(left, right, (((0,), (0,)), ((), ())), preferred_element_type=f32)


def eliminate(start, work_ref, tables_ref, upper_ref, out_ref):
    panel, sub = PANEL, SUB
    tiles = panel // 8
    in_tile = lax.broadcasted_iota(jnp.int32, (8, 128), 0)
    lane_of = lax.broadcasted_iota(jnp.int32, (8, 128), 1)
    far_lane = lax.broadcasted_iota(jnp.int32, (1, 128), 1)
    stop = start + panel
    near = start // 128
    rows = [
        [work_ref[start + 8 * i : start + 8 * i + 8, 128 * t : 128 * t + 128] for i in range(tiles)]
        for t in range(2)
    ]
    scale = [jnp.zeros((8, 128), f32) for i in range(tiles)]
    for begin in range(0, panel, sub):
        lane = start % 128 + begin
        columns = [
            {
                i: jnp.broadcast_to(rows[near][i][:, lane + k : lane + k + 1], (8, 128))
                for i in range((begin + k) // 8, tiles)
            }
            for k in range(sub)
        ]
        cleared = (lane_of >= lane) & (lane_of < lane + sub)
        for i in range(tiles):
            fresh = tables_ref[START + near, start + 8 * i : start + 8 * i + 8, :]
            rows[near][i] = jnp.where(cleared, fresh, rows[near][i])
        for k in range(0, sub, 2):
            row = begin + k
            tile, place = row // 8, row % 8
            one, two = columns[k], columns[k + 1]
            a, b = same_row(one[tile], place), same_row(one[tile], place + 1)
            d = same_row(two[tile], place + 1)
            root = lax.rsqrt(a * d - b * b)
            inverse = root * root
            root_a = lax.rsqrt(a)
            raw = {
                i: (one[i] * d - two[i] * b, two[i] * a - one[i] * b)
                for i in range(tile, tiles)
            }
            below = in_tile > place + 1
            raw[tile] = tuple(jnp.where(below, part, 0.0) for part in raw[tile])
            ratio = {i: (raw[i][0] * inverse, raw[i][1] * inverse) for i in raw}
            for later in range(k + 2, sub):
                other = begin + later
                f = same_row(one[other // 8], other % 8)
                g = same_row(two[other // 8], other % 8)
                for i in range(other // 8, tiles):
                    if later < k + 4:
                        change = (raw[i][0] * f + raw[i][1] * g) * inverse
                    else:
                        change = ratio[i][0] * f + ratio[i][1] * g
                    columns[later][i] = columns[later][i] - change
            ratio[tile] = (
                jnp.where(in_tile == place + 1, b * (root_a * root_a), ratio[tile][0]),
                ratio[tile][1],
            )
            for group in rows:
                f, g = same_row(group[tile], place), same_row(group[tile], place + 1)
                for i in range(tile, tiles):
                    group[i] = group[i] - (ratio[i][0] * f + ratio[i][1] * g)
            scale[tile] = jnp.where(in_tile == place, root_a, scale[tile])
            scale[tile] = jnp.where(in_tile == place + 1, root * (a * root_a), scale[tile])
    solved = [
        jnp.concatenate([group[i] * scale[i] for i in range(tiles)], axis=0) for group in rows
    ]
    for t in range(2):
        lanes = slice(128 * t, 128 * t + 128)
        done = jnp.where(far_lane + 128 * t < stop, solved[t], 0.0)
        for piece in range(panel // 16):
            out_ref[start // 16 + piece, :, lanes] = done[16 * piece : 16 * piece + 16, :]
        if near == 0:
            upper_ref[start:stop, lanes] = solved[t] if t else done
    end = 128 * near + 128
    if stop == end:
        return
    turned, straight = six_products(jnp.concatenate(solved, axis=1))
    change = over_rows(turned[:, 128 * near : end], straight)
    inside = (far_lane + 128 * near >= start) & (far_lane + 128 * near < stop)
    for t in range(2):
        lanes = slice(128 * t, 128 * t + 128)
        kept = work_ref[stop:end, lanes]
        if t == near:
            kept = jnp.where(inside, 0.0, kept)
        work_ref[stop:end, lanes] = kept - change[stop - 128 * near :, lanes]


def refactor_body(
    shares_ref, turned_ref, tables_ref, centers_ref, mixing_ref, evidence_ref,
    out_ref, far_means_ref, far_weights_ref, far_evidence_ref,
    work_ref, upper_ref, means_ref, weights_ref, sent_ref,
):
    position, unused = place()
    vector_total = turned_ref.shape[0] * turned_ref.shape[2]
    share = shares_ref[:, pl.ds(position, 1), :].reshape(16, 128)

    def weighted_parts(pair, half):
        weighted = [
            turned_ref[block, 128 * half : 128 * half + 128, :].astype(f32)
            * share[block : block + 1, :]
            for block in (2 * pair, 2 * pair + 1)
        ]
        return list(three_parts(jnp.concatenate(weighted, axis=1)))

    def vectors_of(pair, first):
        blocks = [turned_ref[block, first:, :] for block in (2 * pair, 2 * pair + 1)]
        return jnp.concatenate(blocks, axis=1)

    def added_up(parts):
        return parts[:128] + parts[128:256] + parts[256:384]

    total = jnp.zeros((432, 256), f32)
    counts = jnp.zeros((16, 128), f32)
    for pair in range(8):
        everyone = jnp.concatenate([shares_ref[2 * pair], shares_ref[2 * pair + 1]], axis=1)
        counts += everyone[:, :128] + everyone[:, 128:]
        stacked = jnp.concatenate(weighted_parts(pair, 0) + list(three_parts(everyone)), axis=0)
        total += over_lanes(stacked, vectors_of(pair, 0))
    gram = added_up(total)
    moments = total[384:400] + total[400:416] + total[416:]
    everyone_of = lax.broadcasted_iota(jnp.int32, (16, 1), 0)
    moment = jnp.sum(jnp.where(everyone_of == position, moments, 0.0), axis=0, keepdims=True)
    count = jnp.sum(jnp.sum(share, axis=0, keepdims=True), axis=1, keepdims=True)
    kept = (1.0 - step_weight) * own_of(mixing_ref, position)
    weight = kept + step_weight * count / vector_total
    center = centers_ref[pl.ds(position, 1), :]
    rows, cols = eye_of(128)
    same = rows == cols
    mean = (kept * center + step_weight * moment / vector_total) / weight

    def down(row):
        return jnp.sum(jnp.where(same, row, 0.0), axis=1, keepdims=True)

    def assembled(gram, half, t):
        mine, lanes = slice(128 * half, 128 * half + 128), slice(128 * t, 128 * t + 128)
        moment_part = (
            (kept * down(center[:, mine])) * center[:, lanes] + (step_weight / vector_total) * gram
        ) / weight - down(mean[:, mine]) * mean[:, lanes]
        if half == t:
            moment_part += jnp.where(same, ridge_term, 0.0)
        return (kept / weight) * tables_ref[SQUARE + t, mine, :] + moment_part * (
            tables_ref[BOTH + t, mine, :]
        )

    for t in range(2):
        lanes = slice(128 * t, 128 * t + 128)
        work_ref[:128, lanes] = assembled(gram[:, lanes], 0, t)
    last = jnp.zeros((384, 128), f32)
    for panel in range(128 // PANEL):
        eliminate(PANEL * panel, work_ref, tables_ref, upper_ref, out_ref)
        if panel < 2:
            for pair in range(4 * panel, 4 * panel + 4):
                stacked = jnp.concatenate(weighted_parts(pair, 1), axis=0)
                last += over_lanes(stacked, vectors_of(pair, 128))
        if panel == 0:
            few = [index[:16, :16] for index in (rows, cols)]
            everyone_at = few[0] == few[1]
            priors = jnp.sum(jnp.where(everyone_at, mixing_ref[...], 0.0), axis=1, keepdims=True)
            all_kept = (1.0 - step_weight) * priors
            counts = jnp.sum(counts, axis=1, keepdims=True)
            weights = all_kept + step_weight * counts / vector_total
            means_ref[...] = (
                all_kept * centers_ref[...] + step_weight * moments / vector_total
            ) / weights
            weights_ref[...] = jnp.sum(
                jnp.where(everyone_at, weights, 0.0), axis=0, keepdims=True
            )
        if panel == 2:
            copies = [
                pltpu.make_async_copy(source, target, sent_ref.at[place_of])
                for place_of, (source, target) in enumerate((
                    (means_ref, far_means_ref),
                    (weights_ref, far_weights_ref),
                    (evidence_ref, far_evidence_ref),
                ))
            ]
            for copy in copies:
                copy.start()
            corner = assembled(added_up(last), 1, 1)
    turned, straight = six_products(upper_ref[...])
    change = over_rows(turned[:, 128:], straight)
    work_ref[128:, :128] = -change[:, :128]
    work_ref[128:, 128:] = corner - change[:, 128:]
    for panel in range(128 // PANEL):
        eliminate(128 + PANEL * panel, work_ref, tables_ref, upper_ref, out_ref)
    for copy in copies:
        copy.wait()


REF_SCRATCH = [
    pltpu.VMEM((256, 256), f32),
    pltpu.VMEM((128, 256), f32),
    pltpu.VMEM((16, 256), f32),
    pltpu.VMEM((1, 16), f32),
    pltpu.SemaphoreType.DMA((3,)),
]


def exchanged(array, axis):
    return lax.all_to_all(array, axis, split_axis=0, concat_axis=0, tiled=True)


def local(vectors, centers, factors, mixing):
    groups, peers = lax.axis_size("dp"), lax.axis_size("comp")
    priors = mixing.reshape(1, 16)
    spread = call(spread_body, shape((groups, 160, 128), bf16), vectors, factors, near=False)
    got = exchanged(spread, "dp")
    other = lax.ppermute(got, "comp", [(i, i ^ 1) for i in range(peers)])
    scores = call(
        score_body, shape((16, 1, 128)), got, other, centers, priors,
        scratch=[pltpu.VMEM((256, 256), bf16)], flops=1 << 29,
    )
    scores, after, after_other = lax.optimization_barrier((scores, got, other))
    scores_here = exchanged(scores, "dp")
    tables, turned = call(
        prepare_body,
        [shape((TABLES, 256, 128)), shape((16, 256, 128), bf16)],
        after, after_other, scratch=INV_SCRATCH, flops=1 << 30,
    )
    scores_here, tables, turned = lax.optimization_barrier((scores_here, tables, turned))
    partial = call(partial_body, shape((peers, 2, 128)), scores_here)
    pairs = exchanged(partial, "comp")
    shares, evidence = call(
        share_body, [shape((groups, 16, 128)), shape((1, 128))], scores_here, pairs
    )
    shares_all = exchanged(shares, "dp")
    refreshed, new_means, new_weights, evidence = call(
        refactor_body, [shape((16, 16, 256)), far((16, 256)), far((1, 16)), far((1, 128))],
        shares_all, turned, tables, centers, priors, evidence, scratch=REF_SCRATCH, flops=1 << 32,
    )
    new_factors = exchanged(refreshed, "dp")
    return new_factors, new_means, new_weights.reshape(16), evidence.reshape(128)


def solution(mesh):
    return jax.shard_map(
        local,
        mesh=mesh,
        in_specs=(P("dp", None), P("comp", None), P("comp", "dp", None), P("comp")),
        out_specs=(P("comp", "dp", None), P("comp", None), P("comp"), P("dp")),
        check_vma=False,
    )
```

time: 105 us -> 104 us (level)
  blocking collectives: 62.9 us -> 77 us
  waiting for transfers between devices: 13.5 us -> 5.21 us
  starting transfers between devices: 10 us -> 5.62 us
  Pallas kernels: 16.3 us -> 14.2 us
    all_to_all x3 -> x4, blocking collectives: 62.9 us -> 77 us  [exchanged(): return lax.all_to_all(array, axis, split_axis=0, concat_axis=0, tiled=True)]
    all_to_all x2 -> x1, waiting for transfers between devices: 11.4 us -> 3.15 us  [exchanged(): return lax.all_to_all(array, axis, split_axis=0, concat_axis=0, tiled=True)]
    all_to_all x2 -> x1, starting transfers between devices: 7.97 us -> 3.58 us  [exchanged(): return lax.all_to_all(array, axis, split_axis=0, concat_axis=0, tiled=True)]
    pallas_call x7 -> x6, Pallas kernels: 16.3 us -> 14.2 us  [call(): pl.pallas_call(body, out_shape=out_shape, in_specs=[vmem] * len(args), ou...]
  transfers between devices with their start and end apart: 3 -> 2, of which waited for: 3 -> 2; matrix products, arithmetic and copies ran while one was open for 0% -> 0% of each run, Pallas kernels for 5% -> 4%
where the time goes in v4:
time: 104 us; the launch traced here: 103 us
  blocking collectives  77 us (74%)
  Pallas kernels  14.2 us (14%)
  starting transfers between devices  5.62 us (5%)
  waiting for transfers between devices  5.21 us (5%)
    all_to_all x4, blocking collectives, exchanged(): return lax.all_to_all(array, axis, split_axis=0, concat_axis=0, tiled=True)  77 us
    pallas_call x6, Pallas kernels, call(): pl.pallas_call(body, out_shape=out_shape, in_specs=[vmem] * len(args), ou...  14.2 us
    all_to_all x1, starting transfers between devices, exchanged(): return lax.all_to_all(array, axis, split_axis=0, concat_axis=0, tiled=True)  3.58 us
    all_to_all x1, waiting for transfers between devices, exchanged(): return lax.all_to_all(array, axis, split_axis=0, concat_axis=0, tiled=True)  3.15 us
  transfers between devices with their start and end apart: 2, of which 2 were waited for; matrix products, arithmetic and copies ran while one was open for 0% of the time, Pallas kernels for 4%

profile of v4, /device:TPU:8, one launch (start us, length us, event | category | flops | bytes accessed | tf_op | source)
XLA Modules:
  0.0 103.4 jit_solution(281231889837080105)
XLA Ops:
  0.6 1.0 %shard_map.75 = bf16[16,160,128]{2,1,0:T(8,128)(2,1)S(1)} custom-call(bf16[128,256]{1,0:T(8,128)(2,1)} %vectors_ref.1, bf16[16,16,256]{2,1,0:T(8,128)(2,1)} %factors_ref.1), custom_call_target="tpu_custom_call" | custom-call | tf_op jit(solution)/shard_map/pallas_call | solution.py:25
  1.7 0.0 copy-start
  1.7 31.1 %all_to_all.25.got_ref = bf16[16,160,128]{2,1,0:T(8,128)(2,1)S(1)} all-to-all(bf16[16,160,128]{2,1,0:T(8,128)(2,1)S(1)} %shard_map.75), channel_id=1, replica_groups=mesh['dp'=16,'comp'=32] {'dp'}, dimensions={0} | all-to-all | bytes 1310720 | tf_op jit(solution)/shard_map/all_to_all | solution.py:400
  32.7 0.0 copy-start.1
  32.7 2.0 %collective-permute-start = (bf16[16,160,128]{2,1,0:T(8,128)(2,1)S(1)}, bf16[16,160,128]{2,1,0:T(8,128)(2,1)S(1)}, u32[]{:S(2)}, u32[]{:S(2)}) collective-permute-start(bf16[16,160,128]{2,1,0:T(8,128)(2,1)S(1)} %all_to_all.25.got_ref), channel_id=1, source_target_pairs={{0,1},{1,0},{2,3},{3,2},{4,5},{5,4},{6,7},{7,6},{8,9},{9,8},{10,11... | collective-permute-start | bytes 1966088 | tf_op jit(solution)/shard_map/ppermute | solution.py:408
  34.8 2.1 %collective-permute-done.other_ref = bf16[16,160,128]{2,1,0:T(8,128)(2,1)S(1)} collective-permute-done((bf16[16,160,128]{2,1,0:T(8,128)(2,1)S(1)}, bf16[16,160,128]{2,1,0:T(8,128)(2,1)S(1)}, u32[]{:S(2)}, u32[]{:S(2)}) %collective-permute-start) | collective-permute-done | bytes 655392 | tf_op jit(solution)/shard_map/ppermute | solution.py:408
  36.9 0.0 copy-done
  36.9 0.0 copy-done.1
  36.9 1.3 %shard_map.76 = f32[16,1,128]{2,1,0:T(1,128)} custom-call(bf16[16,160,128]{2,1,0:T(8,128)(2,1)S(1)} %all_to_all.25.got_ref, bf16[16,160,128]{2,1,0:T(8,128)(2,1)S(1)} %collective-permute-done.other_ref, f32[16,256]{1,0:T(8,128)S(1)} %copy-done, f32[1,16]{1,0:T(1,128)S(1)} %bitcast.3), custom_call_target="tpu_custom_call" | custom-call | flops 536870912 | tf_op jit(solution)/shard_map/pallas_call | solution.py:25
  38.2 3.6 %all-to-all-start.1 = ((f32[16,1,128]{2,1,0:T(1,128)}), f32[16,1,128]{2,1,0:T(1,128)S(1)}, u32[]{:S(2)}, u32[]{:S(2)}) async-start(f32[16,1,128]{2,1,0:T(1,128)} %shard_map.76), calls=%async_computation.1 | async-start | bytes 16384 | tf_op jit(solution)/shard_map/all_to_all | solution.py:400
  41.8 3.9 %shard_map.77 = (f32[6,256,128]{2,1,0:T(8,128)S(1)}, bf16[16,256,128]{2,1,0:T(8,128)(2,1)S(1)}) custom-call(bf16[16,160,128]{2,1,0:T(8,128)(2,1)S(1)} %all_to_all.25.got_ref, bf16[16,160,128]{2,1,0:T(8,128)(2,1)S(1)} %collective-permute-done.other_ref), custom_call_target="tpu_custom_call" | custom-call | flops 1073741824 | tf_op jit(solution)/shard_map/pallas_call | solution.py:25
  45.7 3.2 %all-to-all-done.1.scores_ref = f32[16,1,128]{2,1,0:T(1,128)S(1)} async-done(((f32[16,1,128]{2,1,0:T(1,128)}), f32[16,1,128]{2,1,0:T(1,128)S(1)}, u32[]{:S(2)}, u32[]{:S(2)}) %all-to-all-start.1) | async-done | bytes 8224 | tf_op jit(solution)/shard_map/all_to_all | solution.py:400
  48.9 18.7 %all_to_all.26.pairs_ref = f32[32,2,128]{2,1,0:T(2,128)S(1)} all-to-all(f32[32,2,128]{2,1,0:T(2,128)S(1)} %shard_map.78), channel_id=1, replica_groups=mesh['dp'=16,'comp'=32] {'comp'}, dimensions={0} | all-to-all | bytes 65536 | tf_op jit(solution)/shard_map/all_to_all | solution.py:400
  67.6 0.1 shard_map.79
  67.7 13.1 %all_to_all.27.shares_ref = f32[16,16,128]{2,1,0:T(8,128)S(1)} all-to-all(f32[16,16,128]{2,1,0:T(8,128)S(1)} %get-tuple-element.24), channel_id=1, replica_groups=mesh['dp'=16,'comp'=32] {'dp'}, dimensions={0} | all-to-all | bytes 262144 | tf_op jit(solution)/shard_map/all_to_all | solution.py:400
  80.8 7.8 %shard_map.80 = (f32[16,16,256]{2,1,0:T(8,128)S(1)}, f32[16,256]{1,0:T(8,128)}, f32[1,16]{1,0:T(1,128)}, f32[1,128]{1,0:T(1,128)}) custom-call(f32[16,16,128]{2,1,0:T(8,128)S(1)} %all_to_all.27.shares_ref, bf16[16,256,128]{2,1,0:T(8,128)(2,1)S(1)} %get-tuple-element.25.turned_ref, f32[6,256,128]{2,1,0:T(8,128)S(1)} %get-tuple-element.26.tables_ref, ...), custom_call_target="tpu_custom_call" | custom-call | flops 4294967296 | tf_op jit(solution)/shard_map/pallas_call | solution.py:25
  88.6 14.1 %all_to_all.28 = f32[16,16,256]{2,1,0:T(8,128)S(1)} all-to-all(f32[16,16,256]{2,1,0:T(8,128)S(1)} %get-tuple-element.28), channel_id=1, replica_groups=mesh['dp'=16,'comp'=32] {'dp'}, dimensions={0} | all-to-all | bytes 524288 | tf_op jit(solution)/shard_map/all_to_all | solution.py:400
  102.7 0.7 copy.9
  (1 shorter events, 0.0 us)
Async XLA Ops:
  1.7 35.2 %copy-start = (f32[16,256]{1,0:T(8,128)S(1)}, f32[16,256]{1,0:T(8,128)}, u32[]{:S(2)}) copy-start(f32[16,256]{1,0:T(8,128)} %centers_ref.3) | copy-start | bytes 49156
  32.7 4.1 %copy-start.1 = (f32[16]{0:T(128)S(1)}, f32[16]{0:T(128)}, u32[]{:S(2)}) copy-start(f32[16]{0:T(128)} %param.7) | copy-start | bytes 196
  32.7 4.1 %collective-permute-start = (bf16[16,160,128]{2,1,0:T(8,128)(2,1)S(1)}, bf16[16,160,128]{2,1,0:T(8,128)(2,1)S(1)}, u32[]{:S(2)}, u32[]{:S(2)}) collective-permute-start(bf16[16,160,128]{2,1,0:T(8,128)(2,1)S(1)} %all_to_all.25.got_ref), channel_id=1, source_target_pairs={{0,1},{1,0},{2,3},{3,2},{4,5},{5,4},{6,7},{7,6},{8,9},{9,8},{10,11... | collective-permute-start | bytes 1966088 | tf_op jit(solution)/shard_map/ppermute | solution.py:408
  38.2 10.7 %all-to-all-start.1 = ((f32[16,1,128]{2,1,0:T(1,128)}), f32[16,1,128]{2,1,0:T(1,128)S(1)}, u32[]{:S(2)}, u32[]{:S(2)}) async-start(f32[16,1,128]{2,1,0:T(1,128)} %shard_map.76), calls=%async_computation.1 | async-start | bytes 16384 | tf_op jit(solution)/shard_map/all_to_all | solution.py:400

commit v5 on v4

--- a/solution.py
+++ b/solution.py
@@ -286,9 +286,8 @@
 
 
 def refactor_body(
-    shares_ref, turned_ref, tables_ref, centers_ref, mixing_ref, evidence_ref,
-    out_ref, far_means_ref, far_weights_ref, far_evidence_ref,
-    work_ref, upper_ref, means_ref, weights_ref, sent_ref,
+    shares_ref, turned_ref, tables_ref, centers_ref, mixing_ref,
+    out_ref, means_ref, weights_ref, work_ref, upper_ref,
 ):
     position, unused = place()
     vector_total = turned_ref.shape[0] * turned_ref.shape[2]
@@ -366,16 +365,6 @@
                 jnp.where(everyone_at, weights, 0.0), axis=0, keepdims=True
             )
         if panel == 2:
-            copies = [
-                pltpu.make_async_copy(source, target, sent_ref.at[place_of])
-                for place_of, (source, target) in enumerate((
-                    (means_ref, far_means_ref),
-                    (weights_ref, far_weights_ref),
-                    (evidence_ref, far_evidence_ref),
-                ))
-            ]
-            for copy in copies:
-                copy.start()
             corner = assembled(added_up(last), 1, 1)
     turned, straight = six_products(upper_ref[...])
     change = over_rows(turned[:, 128:], straight)
@@ -383,17 +372,29 @@
     work_ref[128:, 128:] = corner - change[:, 128:]
     for panel in range(128 // PANEL):
         eliminate(128 + PANEL * panel, work_ref, tables_ref, upper_ref, out_ref)
-    for copy in copies:
-        copy.wait()
 
 
 REF_SCRATCH = [
     pltpu.VMEM((256, 256), f32),
     pltpu.VMEM((128, 256), f32),
-    pltpu.VMEM((16, 256), f32),
-    pltpu.VMEM((1, 16), f32),
-    pltpu.SemaphoreType.DMA((3,)),
 ]
+
+
+def close_body(*refs):
+    sources, targets, sent_ref = refs[:4], refs[4:8], refs[8]
+    copies = []
+    for source, target in zip(sources[1:], targets[1:]):
+        copies.append((source, target))
+    for part in range(4):
+        copies.append((sources[0].at[4 * part : 4 * part + 4], targets[0].at[4 * part : 4 * part + 4]))
+    copies = [
+        pltpu.make_async_copy(source, target, sent_ref.at[place_of])
+        for place_of, (source, target) in enumerate(copies)
+    ]
+    for copy in copies:
+        copy.start()
+    for copy in copies:
+        copy.wait()
 
 
 def exchanged(array, axis):
@@ -424,11 +425,15 @@
         share_body, [shape((groups, 16, 128)), shape((1, 128))], scores_here, pairs
     )
     shares_all = exchanged(shares, "dp")
-    refreshed, new_means, new_weights, evidence = call(
-        refactor_body, [shape((16, 16, 256)), far((16, 256)), far((1, 16)), far((1, 128))],
-        shares_all, turned, tables, centers, priors, evidence, scratch=REF_SCRATCH, flops=1 << 32,
-    )
-    new_factors = exchanged(refreshed, "dp")
+    refreshed, new_means, new_weights = call(
+        refactor_body, [shape((16, 16, 256)), shape((16, 256)), shape((1, 16))],
+        shares_all, turned, tables, centers, priors, scratch=REF_SCRATCH, flops=1 << 32,
+    )
+    new_factors, new_means, new_weights, evidence = call(
+        close_body, [far((16, 16, 256)), far((16, 256)), far((1, 16)), far((1, 128))],
+        exchanged(refreshed, "dp"), new_means, new_weights, evidence,
+        scratch=[pltpu.SemaphoreType.DMA((7,))],
+    )
     return new_factors, new_means, new_weights.reshape(16), evidence.reshape(128)
 
 

time: 104 us -> 103 us (level)
    pallas_call x6 -> x7, Pallas kernels: 14.2 us -> 14.3 us  [call(): pl.pallas_call(body, out_shape=out_shape, in_specs=[vmem] * len(args), ou...]
where the time goes in v5:
time: 103 us
  blocking collectives  77 us (75%)
  Pallas kernels  14.3 us (14%)
  starting transfers between devices  5.62 us (5%)
  waiting for transfers between devices  5.21 us (5%)
    all_to_all x4, blocking collectives, exchanged(): return lax.all_to_all(array, axis, split_axis=0, concat_axis=0, tiled=True)  77 us
    pallas_call x7, Pallas kernels, call(): pl.pallas_call(body, out_shape=out_shape, in_specs=[vmem] * len(args), ou...  14.3 us
    all_to_all x1, starting transfers between devices, exchanged(): return lax.all_to_all(array, axis, split_axis=0, concat_axis=0, tiled=True)  3.58 us
    all_to_all x1, waiting for transfers between devices, exchanged(): return lax.all_to_all(array, axis, split_axis=0, concat_axis=0, tiled=True)  3.15 us
    ppermute x1, waiting for transfers between devices, local(): other = lax.ppermute(got, 'comp', [(i, i ^ 1) for i in range(peers)])  2.06 us
  transfers between devices with their start and end apart: 2, of which 2 were waited for; matrix products, arithmetic and copies ran while one was open for 0% of the time, Pallas kernels for 4%

profile of v5, /device:TPU:8, one launch (start us, length us, event | category | flops | bytes accessed | tf_op | source)
XLA Modules:
  0.0 102.9 jit_solution(282204975429736109)
XLA Ops:
  0.6 1.0 %shard_map.75 = bf16[16,160,128]{2,1,0:T(8,128)(2,1)S(1)} custom-call(bf16[128,256]{1,0:T(8,128)(2,1)} %vectors_ref.1, bf16[16,16,256]{2,1,0:T(8,128)(2,1)} %factors_ref.1), custom_call_target="tpu_custom_call" | custom-call | tf_op jit(solution)/shard_map/pallas_call | solution.py:25
  1.7 0.0 copy-start
  1.7 31.1 %all_to_all.25.got_ref = bf16[16,160,128]{2,1,0:T(8,128)(2,1)S(1)} all-to-all(bf16[16,160,128]{2,1,0:T(8,128)(2,1)S(1)} %shard_map.75), channel_id=1, replica_groups=mesh['dp'=16,'comp'=32] {'dp'}, dimensions={0} | all-to-all | bytes 1310720 | tf_op jit(solution)/shard_map/all_to_all | solution.py:401
  32.7 0.0 copy-start.1
  32.7 2.0 %collective-permute-start = (bf16[16,160,128]{2,1,0:T(8,128)(2,1)S(1)}, bf16[16,160,128]{2,1,0:T(8,128)(2,1)S(1)}, u32[]{:S(2)}, u32[]{:S(2)}) collective-permute-start(bf16[16,160,128]{2,1,0:T(8,128)(2,1)S(1)} %all_to_all.25.got_ref), channel_id=1, source_target_pairs={{0,1},{1,0},{2,3},{3,2},{4,5},{5,4},{6,7},{7,6},{8,9},{9,8},{10,11... | collective-permute-start | bytes 1966088 | tf_op jit(solution)/shard_map/ppermute | solution.py:409
  34.8 2.1 %collective-permute-done.other_ref = bf16[16,160,128]{2,1,0:T(8,128)(2,1)S(1)} collective-permute-done((bf16[16,160,128]{2,1,0:T(8,128)(2,1)S(1)}, bf16[16,160,128]{2,1,0:T(8,128)(2,1)S(1)}, u32[]{:S(2)}, u32[]{:S(2)}) %collective-permute-start) | collective-permute-done | bytes 655392 | tf_op jit(solution)/shard_map/ppermute | solution.py:409
  36.9 0.0 copy-done
  36.9 0.0 copy-done.1
  36.9 1.3 %shard_map.76 = f32[16,1,128]{2,1,0:T(1,128)} custom-call(bf16[16,160,128]{2,1,0:T(8,128)(2,1)S(1)} %all_to_all.25.got_ref, bf16[16,160,128]{2,1,0:T(8,128)(2,1)S(1)} %collective-permute-done.other_ref, f32[16,256]{1,0:T(8,128)S(1)} %copy-done, f32[1,16]{1,0:T(1,128)S(1)} %bitcast.3), custom_call_target="tpu_custom_call" | custom-call | flops 536870912 | tf_op jit(solution)/shard_map/pallas_call | solution.py:25
  38.2 3.6 %all-to-all-start.1 = ((f32[16,1,128]{2,1,0:T(1,128)}), f32[16,1,128]{2,1,0:T(1,128)S(1)}, u32[]{:S(2)}, u32[]{:S(2)}) async-start(f32[16,1,128]{2,1,0:T(1,128)} %shard_map.76), calls=%async_computation.1 | async-start | bytes 16384 | tf_op jit(solution)/shard_map/all_to_all | solution.py:401
  41.8 3.9 %shard_map.77 = (f32[6,256,128]{2,1,0:T(8,128)S(1)}, bf16[16,256,128]{2,1,0:T(8,128)(2,1)S(1)}) custom-call(bf16[16,160,128]{2,1,0:T(8,128)(2,1)S(1)} %all_to_all.25.got_ref, bf16[16,160,128]{2,1,0:T(8,128)(2,1)S(1)} %collective-permute-done.other_ref), custom_call_target="tpu_custom_call" | custom-call | flops 1073741824 | tf_op jit(solution)/shard_map/pallas_call | solution.py:25
  45.7 3.2 %all-to-all-done.1.scores_ref = f32[16,1,128]{2,1,0:T(1,128)S(1)} async-done(((f32[16,1,128]{2,1,0:T(1,128)}), f32[16,1,128]{2,1,0:T(1,128)S(1)}, u32[]{:S(2)}, u32[]{:S(2)}) %all-to-all-start.1) | async-done | bytes 8224 | tf_op jit(solution)/shard_map/all_to_all | solution.py:401
  48.9 18.7 %all_to_all.26.pairs_ref = f32[32,2,128]{2,1,0:T(2,128)S(1)} all-to-all(f32[32,2,128]{2,1,0:T(2,128)S(1)} %shard_map.78), channel_id=1, replica_groups=mesh['dp'=16,'comp'=32] {'comp'}, dimensions={0} | all-to-all | bytes 65536 | tf_op jit(solution)/shard_map/all_to_all | solution.py:401
  67.6 0.1 shard_map.79
  67.7 13.1 %all_to_all.27.shares_ref = f32[16,16,128]{2,1,0:T(8,128)S(1)} all-to-all(f32[16,16,128]{2,1,0:T(8,128)S(1)} %get-tuple-element.27), channel_id=1, replica_groups=mesh['dp'=16,'comp'=32] {'dp'}, dimensions={0} | all-to-all | bytes 262144 | tf_op jit(solution)/shard_map/all_to_all | solution.py:401
  80.8 7.2 %shard_map.80 = (f32[16,16,256]{2,1,0:T(8,128)S(1)}, f32[16,256]{1,0:T(8,128)S(1)}, f32[1,16]{1,0:T(1,128)S(1)}) custom-call(f32[16,16,128]{2,1,0:T(8,128)S(1)} %all_to_all.27.shares_ref, bf16[16,256,128]{2,1,0:T(8,128)(2,1)S(1)} %get-tuple-element.28.turned_ref, f32[6,256,128]{2,1,0:T(8,128)S(1)} %get-tuple-element.29.tables_ref, f32[16,256]{1,0:T(8,128)S(1)} %copy-done, ...), custom_call_target="tpu_custom_call" | custom-call | flops 4294967296 | tf_op jit(solution)/shard_map/pallas_call | solution.py:25
  88.0 14.1 %all_to_all.28.refs_0_ = f32[16,16,256]{2,1,0:T(8,128)S(1)} all-to-all(f32[16,16,256]{2,1,0:T(8,128)S(1)} %get-tuple-element.30), channel_id=1, replica_groups=mesh['dp'=16,'comp'=32] {'dp'}, dimensions={0} | all-to-all | bytes 524288 | tf_op jit(solution)/shard_map/all_to_all | solution.py:401
  102.1 0.8 shard_map.81
  (1 shorter events, 0.0 us)
Async XLA Ops:
  1.7 35.2 %copy-start = (f32[16,256]{1,0:T(8,128)S(1)}, f32[16,256]{1,0:T(8,128)}, u32[]{:S(2)}) copy-start(f32[16,256]{1,0:T(8,128)} %centers_ref.3) | copy-start | bytes 49156
  32.7 4.1 %copy-start.1 = (f32[16]{0:T(128)S(1)}, f32[16]{0:T(128)}, u32[]{:S(2)}) copy-start(f32[16]{0:T(128)} %param.7) | copy-start | bytes 196
  32.7 4.1 %collective-permute-start = (bf16[16,160,128]{2,1,0:T(8,128)(2,1)S(1)}, bf16[16,160,128]{2,1,0:T(8,128)(2,1)S(1)}, u32[]{:S(2)}, u32[]{:S(2)}) collective-permute-start(bf16[16,160,128]{2,1,0:T(8,128)(2,1)S(1)} %all_to_all.25.got_ref), channel_id=1, source_target_pairs={{0,1},{1,0},{2,3},{3,2},{4,5},{5,4},{6,7},{7,6},{8,9},{9,8},{10,11... | collective-permute-start | bytes 1966088 | tf_op jit(solution)/shard_map/ppermute | solution.py:409
  38.2 10.7 %all-to-all-start.1 = ((f32[16,1,128]{2,1,0:T(1,128)}), f32[16,1,128]{2,1,0:T(1,128)S(1)}, u32[]{:S(2)}, u32[]{:S(2)}) async-start(f32[16,1,128]{2,1,0:T(1,128)} %shard_map.76), calls=%async_computation.1 | async-start | bytes 16384 | tf_op jit(solution)/shard_map/all_to_all | solution.py:401

commit v6 on v5

--- a/solution.py
+++ b/solution.py
@@ -86,35 +86,42 @@
         factor_ref[16 * peer : 16 * peer + 16, 128:] = got_ref[peer, 144:160, :]
 
 
-def score_body(got_ref, other_ref, centers_ref, mixing_ref, out_ref, factor_ref):
-    position, core = place()
+def factor_body(got_ref, centers_ref, mixing_ref, factor_ref, shifted_ref, constant_ref):
+    position, unused = place()
     gather_factor(got_ref, factor_ref)
     wide = factor_ref[...].astype(f32)
     center = centers_ref[pl.ds(position, 1), :]
     shifted = jnp.sum(wide * center, axis=1, keepdims=True)
+    shifted_ref[...] = jnp.broadcast_to(shifted, (256, 128))
     rows, cols = eye_of(256)
     diagonal = jnp.sum(jnp.where(rows == cols, wide, 0.0), axis=1, keepdims=True)
     log_diag = jnp.sum(jnp.log(diagonal), axis=0, keepdims=True)
     log_mix = jnp.log(own_of(mixing_ref, position))
+    constant_ref[0:1, :] = jnp.broadcast_to(log_diag, (1, 128))
+    constant_ref[1:2, :] = jnp.broadcast_to(log_mix, (1, 128))
+
+
+def score_body(got_ref, other_ref, factor_ref, shifted_ref, constant_ref, out_ref):
+    unused, core = place()
     mine = factor_ref[:, pl.ds(pl.multiple_of(core * 128, 128), 128)]
     rest = factor_ref[:, pl.ds(pl.multiple_of((1 - core) * 128, 128), 128)]
     for pair in range(8):
         ours = got_ref[2 * pair : 2 * pair + 2, :128, :].reshape(256, 128)
         theirs = other_ref[2 * pair : 2 * pair + 2, :128, :].reshape(256, 128)
-        whitened = over_lanes(mine, ours) + over_lanes(rest, theirs)
-        whitened -= shifted
-        density = log_diag - 0.5 * jnp.sum(whitened * whitened, axis=0, keepdims=True)
-        scores = density + log_mix - 256 * normal_offset
-        out_ref[2 * pair] = scores[:, :128]
-        out_ref[2 * pair + 1] = scores[:, 128:]
+        product = over_lanes(mine, ours) + over_lanes(rest, theirs)
+        for block in range(2):
+            whitened = product[:, 128 * block : 128 * block + 128] - shifted_ref[...]
+            density = constant_ref[0:1, :] - 0.5 * jnp.sum(
+                whitened * whitened, axis=0, keepdims=True
+            )
+            out_ref[2 * pair + block] = density + constant_ref[1:2, :] - 256 * normal_offset
 
 
 def apart(left, right, **options):
     return jnp.dot(left, right, precision=exact_mode, preferred_element_type=f32)
 
 
-def invert_body(got_ref, tables_ref, factor_ref, inverse_ref):
-    gather_factor(got_ref, factor_ref)
+def invert_body(factor_ref, tables_ref, inverse_ref):
     rows, cols = eye_of(128)
     factors = []
     for start in (0, 128):
@@ -148,7 +155,7 @@
         tables_ref[place + 1] = table[:, 128:]
 
 
-INV_SCRATCH = [pltpu.VMEM((256, 256), bf16), pltpu.VMEM((2, 128, 128), f32)]
+INV_SCRATCH = [pltpu.VMEM((2, 128, 128), f32)]
 
 
 def order_body(got_ref, other_ref, turned_ref):
@@ -160,8 +167,8 @@
         turned_ref[block, theirs, :] = other_ref[block, :128, :].T
 
 
-def prepare_body(got_ref, other_ref, tables_ref, turned_ref, factor_ref, inverse_ref):
-    invert_body(got_ref, tables_ref, factor_ref, inverse_ref)
+def prepare_body(got_ref, other_ref, factor_ref, tables_ref, turned_ref, inverse_ref):
+    invert_body(factor_ref, tables_ref, inverse_ref)
     order_body(got_ref, other_ref, turned_ref)
 
 
@@ -407,16 +414,19 @@
     spread = call(spread_body, shape((groups, 160, 128), bf16), vectors, factors, near=False)
     got = exchanged(spread, "dp")
     other = lax.ppermute(got, "comp", [(i, i ^ 1) for i in range(peers)])
+    factor, shifted, constant = call(
+        factor_body, [shape((256, 256), bf16), shape((256, 128)), shape((2, 128))],
+        got, centers, priors, flops=1 << 27,
+    )
     scores = call(
-        score_body, shape((16, 1, 128)), got, other, centers, priors,
-        scratch=[pltpu.VMEM((256, 256), bf16)], flops=1 << 29,
+        score_body, shape((16, 1, 128)), got, other, factor, shifted, constant, flops=1 << 29,
     )
     scores, after, after_other = lax.optimization_barrier((scores, got, other))
     scores_here = exchanged(scores, "dp")
     tables, turned = call(
         prepare_body,
         [shape((TABLES, 256, 128)), shape((16, 256, 128), bf16)],
-        after, after_other, scratch=INV_SCRATCH, flops=1 << 30,
+        after, after_other, factor, scratch=INV_SCRATCH, flops=1 << 30,
     )
     scores_here, tables, turned = lax.optimization_barrier((scores_here, tables, turned))
     partial = call(partial_body, shape((peers, 2, 128)), scores_here)

time: 103 us -> 103 us (level)
    pallas_call x7 -> x8, Pallas kernels: 14.3 us -> 14.5 us  [call(): pl.pallas_call(body, out_shape=out_shape, in_specs=[vmem] * len(args), ou...]
where the time goes in v6:
time: 103 us
  blocking collectives  77 us (75%)
  Pallas kernels  14.5 us (14%)
  starting transfers between devices  5.62 us (5%)
  waiting for transfers between devices  5.04 us (5%)
    all_to_all x4, blocking collectives, exchanged(): return lax.all_to_all(array, axis, split_axis=0, concat_axis=0, tiled=True)  77 us
    pallas_call x8, Pallas kernels, call(): pl.pallas_call(body, out_shape=out_shape, in_specs=[vmem] * len(args), ou...  14.5 us
    all_to_all x1, starting transfers between devices, exchanged(): return lax.all_to_all(array, axis, split_axis=0, concat_axis=0, tiled=True)  3.58 us
    all_to_all x1, waiting for transfers between devices, exchanged(): return lax.all_to_all(array, axis, split_axis=0, concat_axis=0, tiled=True)  3.16 us
  transfers between devices with their start and end apart: 2, of which 2 were waited for; matrix products, arithmetic and copies ran while one was open for 0% of the time, Pallas kernels for 4%

profile of v6, /device:TPU:8, one launch (start us, length us, event | category | flops | bytes accessed | tf_op | source)
XLA Modules:
  0.0 102.8 jit_solution(12144723003901534860)
XLA Ops:
  0.6 1.0 %shard_map.75 = bf16[16,160,128]{2,1,0:T(8,128)(2,1)S(1)} custom-call(bf16[128,256]{1,0:T(8,128)(2,1)} %vectors_ref.1, bf16[16,16,256]{2,1,0:T(8,128)(2,1)} %factors_ref.1), custom_call_target="tpu_custom_call" | custom-call | tf_op jit(solution)/shard_map/pallas_call | solution.py:25
  1.7 0.0 copy-start
  1.7 31.1 %all_to_all.25.got_ref = bf16[16,160,128]{2,1,0:T(8,128)(2,1)S(1)} all-to-all(bf16[16,160,128]{2,1,0:T(8,128)(2,1)S(1)} %shard_map.75), channel_id=1, replica_groups=mesh['dp'=16,'comp'=32] {'dp'}, dimensions={0} | all-to-all | bytes 1310720 | tf_op jit(solution)/shard_map/all_to_all | solution.py:408
  32.7 0.0 copy-start.1
  32.7 2.0 %collective-permute-start = (bf16[16,160,128]{2,1,0:T(8,128)(2,1)S(1)}, bf16[16,160,128]{2,1,0:T(8,128)(2,1)S(1)}, u32[]{:S(2)}, u32[]{:S(2)}) collective-permute-start(bf16[16,160,128]{2,1,0:T(8,128)(2,1)S(1)} %all_to_all.25.got_ref), channel_id=1, source_target_pairs={{0,1},{1,0},{2,3},{3,2},{4,5},{5,4},{6,7},{7,6},{8,9},{9,8},{10,11... | collective-permute-start | bytes 1966088 | tf_op jit(solution)/shard_map/ppermute | solution.py:416
  34.8 0.0 copy-done
  34.8 0.0 copy-done.1
  34.8 0.2 shard_map.76
  35.0 1.9 %collective-permute-done.other_ref = bf16[16,160,128]{2,1,0:T(8,128)(2,1)S(1)} collective-permute-done((bf16[16,160,128]{2,1,0:T(8,128)(2,1)S(1)}, bf16[16,160,128]{2,1,0:T(8,128)(2,1)S(1)}, u32[]{:S(2)}, u32[]{:S(2)}) %collective-permute-start) | collective-permute-done | bytes 655392 | tf_op jit(solution)/shard_map/ppermute | solution.py:416
  36.9 1.3 %shard_map.77 = f32[16,1,128]{2,1,0:T(1,128)} custom-call(bf16[16,160,128]{2,1,0:T(8,128)(2,1)S(1)} %all_to_all.25.got_ref, bf16[16,160,128]{2,1,0:T(8,128)(2,1)S(1)} %collective-permute-done.other_ref, bf16[256,256]{1,0:T(8,128)(2,1)S(1)} %get-tuple-element.24.factor_ref, f32[256,128]{1,0:T(8,128)S(1)} %get-tuple-element.25.shifted_ref, ...), custom_call_target="tpu_custom_call" | custom-call | flops 536870912 | tf_op jit(solution)/shard_map/pallas_call | solution.py:25
  38.2 3.6 %all-to-all-start.1 = ((f32[16,1,128]{2,1,0:T(1,128)}), f32[16,1,128]{2,1,0:T(1,128)S(1)}, u32[]{:S(2)}, u32[]{:S(2)}) async-start(f32[16,1,128]{2,1,0:T(1,128)} %shard_map.77), calls=%async_computation.1 | async-start | bytes 16384 | tf_op jit(solution)/shard_map/all_to_all | solution.py:408
  41.8 3.9 %shard_map.78 = (f32[6,256,128]{2,1,0:T(8,128)S(1)}, bf16[16,256,128]{2,1,0:T(8,128)(2,1)S(1)}) custom-call(bf16[16,160,128]{2,1,0:T(8,128)(2,1)S(1)} %all_to_all.25.got_ref, bf16[16,160,128]{2,1,0:T(8,128)(2,1)S(1)} %collective-permute-done.other_ref, bf16[256,256]{1,0:T(8,128)(2,1)S(1)} %get-tuple-element.24.factor_ref), custom_call_target="tpu_custom_call" | custom-call | flops 1073741824 | tf_op jit(solution)/shard_map/pallas_call | solution.py:25
  45.7 3.2 %all-to-all-done.1.scores_ref = f32[16,1,128]{2,1,0:T(1,128)S(1)} async-done(((f32[16,1,128]{2,1,0:T(1,128)}), f32[16,1,128]{2,1,0:T(1,128)S(1)}, u32[]{:S(2)}, u32[]{:S(2)}) %all-to-all-start.1) | async-done | bytes 8224 | tf_op jit(solution)/shard_map/all_to_all | solution.py:408
  48.9 18.7 %all_to_all.26.pairs_ref = f32[32,2,128]{2,1,0:T(2,128)S(1)} all-to-all(f32[32,2,128]{2,1,0:T(2,128)S(1)} %shard_map.79), channel_id=1, replica_groups=mesh['dp'=16,'comp'=32] {'comp'}, dimensions={0} | all-to-all | bytes 65536 | tf_op jit(solution)/shard_map/all_to_all | solution.py:408
  67.6 0.1 shard_map.80
  67.7 13.1 %all_to_all.27.shares_ref = f32[16,16,128]{2,1,0:T(8,128)S(1)} all-to-all(f32[16,16,128]{2,1,0:T(8,128)S(1)} %get-tuple-element.33), channel_id=1, replica_groups=mesh['dp'=16,'comp'=32] {'dp'}, dimensions={0} | all-to-all | bytes 262144 | tf_op jit(solution)/shard_map/all_to_all | solution.py:408
  80.8 7.2 %shard_map.81 = (f32[16,16,256]{2,1,0:T(8,128)S(1)}, f32[16,256]{1,0:T(8,128)S(1)}, f32[1,16]{1,0:T(1,128)S(1)}) custom-call(f32[16,16,128]{2,1,0:T(8,128)S(1)} %all_to_all.27.shares_ref, bf16[16,256,128]{2,1,0:T(8,128)(2,1)S(1)} %get-tuple-element.34.turned_ref, f32[6,256,128]{2,1,0:T(8,128)S(1)} %get-tuple-element.35.tables_ref, f32[16,256]{1,0:T(8,128)S(1)} %copy-done, ...), custom_call_target="tpu_custom_call" | custom-call | flops 4294967296 | tf_op jit(solution)/shard_map/pallas_call | solution.py:25
  88.0 14.1 %all_to_all.28.refs_0_ = f32[16,16,256]{2,1,0:T(8,128)S(1)} all-to-all(f32[16,16,256]{2,1,0:T(8,128)S(1)} %get-tuple-element.36), channel_id=1, replica_groups=mesh['dp'=16,'comp'=32] {'dp'}, dimensions={0} | all-to-all | bytes 524288 | tf_op jit(solution)/shard_map/all_to_all | solution.py:408
  102.1 0.8 shard_map.82
  (1 shorter events, 0.0 us)
Async XLA Ops:
  1.7 33.1 %copy-start = (f32[16,256]{1,0:T(8,128)S(1)}, f32[16,256]{1,0:T(8,128)}, u32[]{:S(2)}) copy-start(f32[16,256]{1,0:T(8,128)} %centers_ref.3) | copy-start | bytes 49156
  32.7 2.1 %copy-start.1 = (f32[16]{0:T(128)S(1)}, f32[16]{0:T(128)}, u32[]{:S(2)}) copy-start(f32[16]{0:T(128)} %param.7) | copy-start | bytes 196
  32.7 4.1 %collective-permute-start = (bf16[16,160,128]{2,1,0:T(8,128)(2,1)S(1)}, bf16[16,160,128]{2,1,0:T(8,128)(2,1)S(1)}, u32[]{:S(2)}, u32[]{:S(2)}) collective-permute-start(bf16[16,160,128]{2,1,0:T(8,128)(2,1)S(1)} %all_to_all.25.got_ref), channel_id=1, source_target_pairs={{0,1},{1,0},{2,3},{3,2},{4,5},{5,4},{6,7},{7,6},{8,9},{9,8},{10,11... | collective-permute-start | bytes 1966088 | tf_op jit(solution)/shard_map/ppermute | solution.py:416
  38.2 10.7 %all-to-all-start.1 = ((f32[16,1,128]{2,1,0:T(1,128)}), f32[16,1,128]{2,1,0:T(1,128)S(1)}, u32[]{:S(2)}, u32[]{:S(2)}) async-start(f32[16,1,128]{2,1,0:T(1,128)} %shard_map.77), calls=%async_computation.1 | async-start | bytes 16384 | tf_op jit(solution)/shard_map/all_to_all | solution.py:408

commit v7 on v6

--- a/solution.py
+++ b/solution.py
@@ -86,7 +86,9 @@
         factor_ref[16 * peer : 16 * peer + 16, 128:] = got_ref[peer, 144:160, :]
 
 
-def factor_body(got_ref, centers_ref, mixing_ref, factor_ref, shifted_ref, constant_ref):
+def factor_body(
+    got_ref, centers_ref, mixing_ref, factor_ref, shifted_ref, constant_ref, tables_ref, inverse_ref
+):
     position, unused = place()
     gather_factor(got_ref, factor_ref)
     wide = factor_ref[...].astype(f32)
@@ -99,10 +101,12 @@
     log_mix = jnp.log(own_of(mixing_ref, position))
     constant_ref[0:1, :] = jnp.broadcast_to(log_diag, (1, 128))
     constant_ref[1:2, :] = jnp.broadcast_to(log_mix, (1, 128))
-
-
-def score_body(got_ref, other_ref, factor_ref, shifted_ref, constant_ref, out_ref):
+    invert_body(factor_ref, tables_ref, inverse_ref)
+
+
+def score_body(got_ref, other_ref, factor_ref, shifted_ref, constant_ref, out_ref, turned_ref):
     unused, core = place()
+    order_body(got_ref, other_ref, turned_ref)
     mine = factor_ref[:, pl.ds(pl.multiple_of(core * 128, 128), 128)]
     rest = factor_ref[:, pl.ds(pl.multiple_of((1 - core) * 128, 128), 128)]
     for pair in range(8):
@@ -165,11 +169,6 @@
     for block in range(16):
         turned_ref[block, ours, :] = got_ref[block, :128, :].T
         turned_ref[block, theirs, :] = other_ref[block, :128, :].T
-
-
-def prepare_body(got_ref, other_ref, factor_ref, tables_ref, turned_ref, inverse_ref):
-    invert_body(factor_ref, tables_ref, inverse_ref)
-    order_body(got_ref, other_ref, turned_ref)
 
 
 def partial_body(scores_ref, out_ref):
@@ -414,21 +413,16 @@
     spread = call(spread_body, shape((groups, 160, 128), bf16), vectors, factors, near=False)
     got = exchanged(spread, "dp")
     other = lax.ppermute(got, "comp", [(i, i ^ 1) for i in range(peers)])
-    factor, shifted, constant = call(
-        factor_body, [shape((256, 256), bf16), shape((256, 128)), shape((2, 128))],
-        got, centers, priors, flops=1 << 27,
-    )
-    scores = call(
-        score_body, shape((16, 1, 128)), got, other, factor, shifted, constant, flops=1 << 29,
-    )
-    scores, after, after_other = lax.optimization_barrier((scores, got, other))
+    factor, shifted, constant, tables = call(
+        factor_body,
+        [shape((256, 256), bf16), shape((256, 128)), shape((2, 128)), shape((TABLES, 256, 128))],
+        got, centers, priors, scratch=INV_SCRATCH, flops=1 << 27,
+    )
+    scores, turned = call(
+        score_body, [shape((16, 1, 128)), shape((16, 256, 128), bf16)],
+        got, other, factor, shifted, constant, flops=1 << 29,
+    )
     scores_here = exchanged(scores, "dp")
-    tables, turned = call(
-        prepare_body,
-        [shape((TABLES, 256, 128)), shape((16, 256, 128), bf16)],
-        after, after_other, factor, scratch=INV_SCRATCH, flops=1 << 30,
-    )
-    scores_here, tables, turned = lax.optimization_barrier((scores_here, tables, turned))
     partial = call(partial_body, shape((peers, 2, 128)), scores_here)
     pairs = exchanged(partial, "comp")
     shares, evidence = call(

time: 103 us -> 104 us (level)
  blocking collectives: 77 us -> 87 us
  waiting for transfers between devices: 5.04 us -> 0.01 us
  starting transfers between devices: 5.62 us -> 2.04 us
    all_to_all x4 -> x5, blocking collectives: 77 us -> 87 us  [exchanged(): return lax.all_to_all(array, axis, split_axis=0, concat_axis=0, tiled=True)]
    all_to_all x1 -> x0, starting transfers between devices: 3.58 us -> none  [exchanged(): return lax.all_to_all(array, axis, split_axis=0, concat_axis=0, tiled=True)]
    all_to_all x1 -> x0, waiting for transfers between devices: 3.16 us -> none  [exchanged(): return lax.all_to_all(array, axis, split_axis=0, concat_axis=0, tiled=True)]
    ppermute x1, waiting for transfers between devices: 1.88 us -> 0.01 us  [local(): other = lax.ppermute(got, 'comp', [(i, i ^ 1) for i in range(peers)])]
    pallas_call x8 -> x7, Pallas kernels: 14.5 us -> 13.7 us  [call(): pl.pallas_call(body, out_shape=out_shape, in_specs=[vmem] * len(args), ou...]
  transfers between devices with their start and end apart: 2 -> 1, of which waited for: 2 -> 0; matrix products, arithmetic and copies ran while one was open for 0% -> 0% of each run, Pallas kernels for 4% -> 4%
where the time goes in v7:
time: 104 us
  blocking collectives  87 us (84%)
  Pallas kernels  13.7 us (13%)
  starting transfers between devices  2.04 us (2%)
    all_to_all x5, blocking collectives, exchanged(): return lax.all_to_all(array, axis, split_axis=0, concat_axis=0, tiled=True)  87 us
    pallas_call x7, Pallas kernels, call(): pl.pallas_call(body, out_shape=out_shape, in_specs=[vmem] * len(args), ou...  13.7 us
  transfers between devices with their start and end apart: 1, of which 0 were waited for; matrix products, arithmetic and copies ran while one was open for 0% of the time, Pallas kernels for 4%

profile of v7, /device:TPU:8, one launch (start us, length us, event | category | flops | bytes accessed | tf_op | source)
XLA Modules:
  0.0 103.5 jit_solution(4312608438532428411)
XLA Ops:
  0.6 1.0 %shard_map.75 = bf16[16,160,128]{2,1,0:T(8,128)(2,1)S(1)} custom-call(bf16[128,256]{1,0:T(8,128)(2,1)} %vectors_ref.1, bf16[16,16,256]{2,1,0:T(8,128)(2,1)} %factors_ref.1), custom_call_target="tpu_custom_call" | custom-call | tf_op jit(solution)/shard_map/pallas_call | solution.py:25
  1.7 0.0 copy-start
  1.7 31.1 %all_to_all.25.got_ref = bf16[16,160,128]{2,1,0:T(8,128)(2,1)S(1)} all-to-all(bf16[16,160,128]{2,1,0:T(8,128)(2,1)S(1)} %shard_map.75), channel_id=1, replica_groups=mesh['dp'=16,'comp'=32] {'dp'}, dimensions={0} | all-to-all | bytes 1310720 | tf_op jit(solution)/shard_map/all_to_all | solution.py:407
  32.7 0.0 copy-start.1
  32.7 2.0 %collective-permute-start = (bf16[16,160,128]{2,1,0:T(8,128)(2,1)S(1)}, bf16[16,160,128]{2,1,0:T(8,128)(2,1)S(1)}, u32[]{:S(2)}, u32[]{:S(2)}) collective-permute-start(bf16[16,160,128]{2,1,0:T(8,128)(2,1)S(1)} %all_to_all.25.got_ref), channel_id=1, source_target_pairs={{0,1},{1,0},{2,3},{3,2},{4,5},{5,4},{6,7},{7,6},{8,9},{9,8},{10,11... | collective-permute-start | bytes 1966088 | tf_op jit(solution)/shard_map/ppermute | solution.py:415
  34.8 0.0 copy-done
  34.8 0.0 copy-done.1
  34.8 4.0 %shard_map.76 = (bf16[256,256]{1,0:T(8,128)(2,1)S(1)}, f32[256,128]{1,0:T(8,128)S(1)}, f32[2,128]{1,0:T(2,128)S(1)}, f32[6,256,128]{2,1,0:T(8,128)S(1)}) custom-call(bf16[16,160,128]{2,1,0:T(8,128)(2,1)S(1)} %all_to_all.25.got_ref, f32[16,256]{1,0:T(8,128)S(1)} %copy-done, f32[1,16]{1,0:T(1,128)S(1)} %bitcast.3), custom_call_target="tpu_custom_call" | custom-call | flops 134217728 | tf_op jit(solution)/shard_map/pallas_call | solution.py:25
  38.8 0.0 collective-permute-done.other_ref
  38.8 0.7 shard_map.77
  39.5 10.6 %all_to_all.26.scores_ref = f32[16,1,128]{2,1,0:T(1,128)S(1)} all-to-all(f32[16,1,128]{2,1,0:T(1,128)S(1)} %get-tuple-element.22), channel_id=1, replica_groups=mesh['dp'=16,'comp'=32] {'dp'}, dimensions={0} | all-to-all | bytes 16384 | tf_op jit(solution)/shard_map/all_to_all | solution.py:407
  50.1 18.7 %all_to_all.27.pairs_ref = f32[32,2,128]{2,1,0:T(2,128)S(1)} all-to-all(f32[32,2,128]{2,1,0:T(2,128)S(1)} %shard_map.78), channel_id=1, replica_groups=mesh['dp'=16,'comp'=32] {'comp'}, dimensions={0} | all-to-all | bytes 65536 | tf_op jit(solution)/shard_map/all_to_all | solution.py:407
  68.8 0.1 shard_map.79
  68.9 12.8 %all_to_all.28.shares_ref = f32[16,16,128]{2,1,0:T(8,128)S(1)} all-to-all(f32[16,16,128]{2,1,0:T(8,128)S(1)} %get-tuple-element.23), channel_id=1, replica_groups=mesh['dp'=16,'comp'=32] {'dp'}, dimensions={0} | all-to-all | bytes 262144 | tf_op jit(solution)/shard_map/all_to_all | solution.py:407
  81.7 7.2 %shard_map.80 = (f32[16,16,256]{2,1,0:T(8,128)S(1)}, f32[16,256]{1,0:T(8,128)S(1)}, f32[1,16]{1,0:T(1,128)S(1)}) custom-call(f32[16,16,128]{2,1,0:T(8,128)S(1)} %all_to_all.28.shares_ref, bf16[16,256,128]{2,1,0:T(8,128)(2,1)S(1)} %get-tuple-element.24.turned_ref, f32[6,256,128]{2,1,0:T(8,128)S(1)} %get-tuple-element.25.tables_ref, f32[16,256]{1,0:T(8,128)S(1)} %copy-done, ...), custom_call_target="tpu_custom_call" | custom-call | flops 4294967296 | tf_op jit(solution)/shard_map/pallas_call | solution.py:25
  88.9 13.9 %all_to_all.29.refs_0_ = f32[16,16,256]{2,1,0:T(8,128)S(1)} all-to-all(f32[16,16,256]{2,1,0:T(8,128)S(1)} %get-tuple-element.26), channel_id=1, replica_groups=mesh['dp'=16,'comp'=32] {'dp'}, dimensions={0} | all-to-all | bytes 524288 | tf_op jit(solution)/shard_map/all_to_all | solution.py:407
  102.7 0.8 shard_map.81
  (1 shorter events, 0.0 us)
Async XLA Ops:
  1.7 33.1 %copy-start = (f32[16,256]{1,0:T(8,128)S(1)}, f32[16,256]{1,0:T(8,128)}, u32[]{:S(2)}) copy-start(f32[16,256]{1,0:T(8,128)} %centers_ref.3) | copy-start | bytes 49156
  32.7 2.1 %copy-start.1 = (f32[16]{0:T(128)S(1)}, f32[16]{0:T(128)}, u32[]{:S(2)}) copy-start(f32[16]{0:T(128)} %param.7) | copy-start | bytes 196
  32.7 6.0 %collective-permute-start = (bf16[16,160,128]{2,1,0:T(8,128)(2,1)S(1)}, bf16[16,160,128]{2,1,0:T(8,128)(2,1)S(1)}, u32[]{:S(2)}, u32[]{:S(2)}) collective-permute-start(bf16[16,160,128]{2,1,0:T(8,128)(2,1)S(1)} %all_to_all.25.got_ref), channel_id=1, source_target_pairs={{0,1},{1,0},{2,3},{3,2},{4,5},{5,4},{6,7},{7,6},{8,9},{9,8},{10,11... | collective-permute-start | bytes 1966088 | tf_op jit(solution)/shard_map/ppermute | solution.py:415
